TPU v7x, 256 devices: a whole 4x4x8 slice. The times are simulated.
256 devices in a mesh: rows: 64 (over y, z, core), cols: 4 (over x).
Axes of the slice: x: 4, y: 4, z: 8, core: 2. Of those that a mesh axis runs over, the one named last changes fastest.
Arguments:
- panel: float32 [131072, 256], P(('rows', 'cols')), may hold values from -17 to 17, as said below
- trailing: float32 [131072, 2048], P('rows', 'cols'), may hold values from -6 to 6
Outputs:
- rfactor: float32 [256, 256], replicated
- projected: float32 [256, 2048], P(None, 'cols')
- updated: float32 [131072, 2048], P('rows', 'cols')
Inputs may be any that keep to these rules, and one draw needn't show every extreme that they name: The panel has full column rank with a moderate condition number (under 100); each column has its own scale and a part shared by all columns.
All inputs are finite; a program needn't handle non-finite values.
Results may differ from a plain program's by a relative error of at most 0.000078.
Values sent between devices are 32-bit elements; how exact they have to be, the bound alone decides.
No kernel may reach another device: no remote copies, remote signals or barrier semaphores. Data moves between devices by JAX's collectives and lax.ppermute only.
A program may use at most 64 MiB of HBM per device.

v0:
```python
import jax
import jax.numpy as jnp
from jax import lax
from jax.sharding import PartitionSpec as P


def joined_along(tiles, dim):
    tiles = jnp.moveaxis(tiles, 0, dim)
    shape = tiles.shape
    return tiles.reshape(*shape[:dim], shape[dim] * shape[dim + 1], *shape[dim + 2 :])


def copy_for_each(array, axis):
    copies = jnp.broadcast_to(array, (lax.axis_size(axis), *array.shape))
    return lax.all_to_all(copies, axis, split_axis=0, concat_axis=0, tiled=True)


def gather_directly(array, axis, dim):
    return joined_along(copy_for_each(array, axis), dim)


def in_one(arrays, axis):
    ends = [0]
    for a in arrays:
        ends.append(ends[-1] + a.size)
    running = lax.psum(jnp.concatenate([a.ravel() for a in arrays]), axis)
    return tuple((running[b:e].reshape(a.shape) for a, b, e in zip(arrays, ends, ends[1:])))


def inner(left, right):
    return lax.dot_general(
        left,
        right,
        (((0,), (0,)), ((), ())),
        precision=lax.Precision.HIGHEST,
        preferred_element_type=jnp.float32,
    )


def times(left, right):
    return jnp.dot(left, right, precision=lax.Precision.HIGHEST, preferred_element_type=jnp.float32)


def lower_solve(rfactor, right):
    return jax.scipy.linalg.solve_triangular(rfactor.T, right, lower=True)


def shards(panel, trailing):
    block = gather_directly(panel, "cols", 0)
    gram, cross = in_one((inner(block, block), inner(block, trailing)), "rows")
    rfactor = jnp.linalg.cholesky(gram).T
    basis = lower_solve(rfactor, block.T).T
    projected = lower_solve(rfactor, cross)
    updated = trailing - times(basis, projected)
    return (rfactor, projected, updated)


def solution(mesh):
    placed = (P(("rows", "cols"), None), P("rows", "cols"))
    return jax.shard_map(
        shards,
        mesh=mesh,
        in_specs=placed,
        out_specs=(P(), P(None, "cols"), P("rows", "cols")),
        check_vma=False,
    )
```

profile of v0, /device:TPU:1, one launch (start us, length us, event | category | flops | bytes accessed | tf_op | source)
XLA Modules:
  0.0 313.1 jit_solution(15103172928544927577)
XLA Ops:
  7.2 0.0 all-reduce.3.cloned.1.call-start
  7.2 1.2 broadcast_in_dim.5
  8.4 30.0 %all_to_all.5 = f32[4,512,256]{2,1,0:T(8,128)S(1)} all-to-all(f32[4,512,256]{2,1,0:T(8,128)S(1)} %broadcast_in_dim.5), channel_id=1, replica_groups=mesh['rows'=64,'cols'=4] {'cols'}, dimensions={0} | all-to-all | bytes 4194304 | tf_op jit(solution)/shard_map/all_to_all | solution.py:15
  38.4 0.0 copy-start
  38.4 3.5 %convolution_bitcast_fusion.1 = f32[32,2,8,128]{3,2,1,0:T(8,128)S(1)} fusion(f32[4,512,256]{2,1,0:T(8,128)S(1)} %all_to_all.5), kind=kOutput, calls=%fused_computation.9 | convolution fusion | flops 1610612736 | bytes 2359296 | tf_op jit(solution)/shard_map/dot_general | solution.py:31
  41.9 0.1 copy.12
  42.1 0.0 copy-done
  42.1 3.7 %convolution_bitcast_fusion = f32[32,4,8,128]{3,2,1,0:T(8,128)S(1)} fusion(f32[2048,256]{1,0:T(8,128)S(1)} %bitcast.53, f32[2048,512]{1,0:T(8,128)S(1)} %copy-done), kind=kOutput, calls=%fused_computation.7 | convolution fusion | flops 3221225472 | bytes 6815744 | tf_op jit(solution)/shard_map/dot_general | solution.py:31
  45.8 0.1 copy.13
  45.9 0.9 pad_maximum_fusion
  46.8 0.0 all-reduce.3.cloned.1.call-update
  46.9 186.6 %all-reduce.3.cloned.1.call-done = f32[196608]{0:T(1024)} async-done(((f32[196608]{0:T(1024)}), f32[196608]{0:T(1024)}) %all-reduce.3.cloned.1.call-update) | async-done | bytes 786448 | tf_op jit(solution)/shard_map/psum | solution.py:26
  233.4 1.2 fusion.18
  234.7 0.1 slice.101
  234.7 0.1 copy.9
  234.9 11.7 %cholesky.50 = f32[128,128]{1,0:T(8,128)S(1)} custom-call(f32[128,128]{1,0:T(8,128)S(1)} %cholesky.118), custom_call_target="Cholesky" | custom-call | tf_op jit(solution)/shard_map/jit(cholesky)/cholesky | solution.py:51
  246.7 9.9 %custom-call.18 = f32[1,128,128]{1,2,0:T(8,128)S(1)} custom-call(f32[1,128,128]{2,1,0:T(8,128)S(1)} %get-tuple-element.35), custom_call_target="InvertDiagBlocksLowerTriangular" | custom-call | tf_op jit(solution)/shard_map/jit(cholesky)/cholesky | solution.py:51
  256.6 0.2 constant_dynamic-update-slice_fusion.1
  256.8 0.3 convolution_subtract_fusion.3
  257.1 11.7 %cholesky.105 = f32[128,128]{1,0:T(8,128)S(1)} custom-call(f32[128,128]{1,0:T(8,128)S(1)} %convolution_subtract_fusion.3), custom_call_target="Cholesky" | custom-call | tf_op jit(solution)/shard_map/jit(cholesky)/cholesky | solution.py:51
  268.9 0.6 compare_reduce_fusion
  270.8 0.8 copy.10
  271.7 0.1 triangular_solve.61
  271.7 4.0 %while.1 = (s32[]{:T(128)}, f32[256,256]{1,0:T(8,128)S(1)}, s32[2,2]{1,0:T(2,128)S(1)}, f32[2,128,128]{2,1,0:T(8,128)S(1)}, s32[]{:T(128)}) while((s32[]{:T(128)}, f32[256,256]{1,0:T(8,128)S(1)}, s32[2,2]{1,0:T(2,128)S(1)}, f32[2,128,128]{2,1,0:T(8,128)S(1)}, s32[]{:T(128)}) %tuple.32), condition=%wide.while_cond, body=%wide.while_body.sunk | while | flops 2 | bytes 131189 | solution.py:45
  271.8 0.6 fusion.32
  272.3 1.4 bitcast_dynamic-update-slice_fusion.2
  273.8 0.6 fusion.32
  274.3 1.4 bitcast_dynamic-update-slice_fusion.2
  275.7 19.9 %custom-call.19 = f32[2,128,128]{1,2,0:T(8,128)S(1)} custom-call(f32[2,128,128]{2,1,0:T(8,128)S(1)} %get-tuple-element.10), custom_call_target="InvertDiagBlocksLowerTriangular" | custom-call | tf_op jit(solution)/shard_map/jit(_solve_triangular)/triangular_solve | solution.py:45
  295.7 0.4 fusion.11
  296.1 0.4 convolution_subtract_fusion.2
  296.5 0.4 fusion.13
  297.0 0.0 copy-start.2
  297.0 1.1 fusion.3
  298.1 0.0 copy-start.1
  298.1 1.8 convolution_subtract_fusion.1
  299.9 1.1 fusion.12
  301.0 0.0 copy-done.2
  301.0 0.0 copy-done.1
  301.0 5.2 %convolution_subtract_fusion = f32[2048,512]{1,0:T(8,128)} fusion(f32[2048,512]{1,0:T(8,128)S(1)} %copy-done.1, f32[256,512]{1,0:T(8,128)S(1)} %pad_maximum_fusion.1, f32[128,2048]{1,0:T(8,128)S(1)} %fusion.12, f32[128,2048]{1,0:T(8,128)S(1)} %fusion.3), kind=kOutput, calls=%fused_computation.2 | convolution fusion | flops 3222798336 | bytes 11010048 | tf_op jit(solution)/shard_map/dot_general | solution.py:41
  (13 shorter events, 0.3 us)
Async XLA Ops:
  7.2 226.3 %all-reduce.3.cloned.1.call-start = ((), (), s32[]{:S(2)}) async-start(), calls=%async_computation.1 | async-start | bytes 1572864 | tf_op jit(solution)/shard_map/psum | solution.py:26
  38.4 3.6 %copy-start = (f32[2048,512]{1,0:T(8,128)S(1)}, f32[2048,512]{1,0:T(8,128)}, u32[]{:S(2)}) copy-start(f32[2048,512]{1,0:T(8,128)} %param.3) | copy-start | bytes 12582916
  297.0 4.0 %copy-start.2 = (f32[256,512]{1,0:T(8,128)}, f32[256,512]{1,0:T(8,128)S(1)}, u32[]{:S(2)}) copy-start(f32[256,512]{1,0:T(8,128)S(1)} %pad_maximum_fusion.1) | copy-start | bytes 1572868
  298.1 2.9 copy-start.1
Sparse Core Ops, SparseCore 0:
  47.0 186.4 all-reduce.2
where the time goes:
time: 314 us; the launch traced here: 313 us
  waiting for transfers between devices  187 us (60%)
  other arithmetic  55 us (18%)
  blocking collectives  30 us (10%)
  matrix products  18 us (6%)
  between operations  15.6 us (5%)
  local copies, waits for them, and re-layouts  7.82 us (2%)
    psum x1, waiting for transfers between devices, in_one(): running = lax.psum(jnp.concatenate([a.ravel() for a in arrays]), axis)  187 us
    another operation x6, other arithmetic, shards(): rfactor = jnp.linalg.cholesky(gram).T  34.1 us
    all_to_all x1, blocking collectives, copy_for_each(): return lax.all_to_all(copies, axis, split_axis=0, concat_axis=0, tiled=True)  30 us
    another operation x4, other arithmetic, lower_solve(): return jax.scipy.linalg.solve_triangular(rfactor.T, right, lower=True)  20 us
    dot_general x2, matrix products, inner(): lax.dot_general(left, right, (((0,), (0,)), ((), ())), precision=lax.Prec...  7.15 us
  transfers between devices with their start and end apart: 1, of which 1 were waited for; matrix products, arithmetic and copies ran while one was open for 0% of the time, Pallas kernels for 0%

commit v1 on v0

v1 whole, which is shorter than its diff:
```python
import jax
import jax.numpy as jnp
from jax import lax
from jax.experimental import pallas as pl
from jax.experimental.pallas import tpu as pltpu
from jax.sharding import PartitionSpec as P

NY, NZ, NC, NX = 4, 8, 2, 4
HIGHEST = lax.Precision.HIGHEST
F32 = jnp.float32


def row_id(y, z, c):
    return (y * NZ + z) * NC + c


GROUP_Y = [[row_id(y, z, c) for y in range(NY)] for z in range(NZ) for c in range(NC)]
GROUP_Z = [[row_id(y, z, c) for z in range(NZ)] for y in range(NY) for c in range(NC)]
CORE_SWAP = [(i, i ^ 1) for i in range(NY * NZ * NC)]
X_UP = [(i, (i + 1) % NX) for i in range(NX)]
X_DOWN = [(i, (i - 1) % NX) for i in range(NX)]


def dot(a, b, dims=((1,), (0,)), precision=HIGHEST):
    return lax.dot_general(a, b, (dims, ((), ())), precision=precision, preferred_element_type=F32)


def exchange(a, axis, groups=None):
    return lax.all_to_all(a, axis, 0, 0, axis_index_groups=groups, tiled=True)


def copies(a, n):
    return jnp.broadcast_to(a[None], (n, *a.shape))


def factor_block(d):
    n = 128
    slabs = n // 8
    D = [d[8 * s : 8 * s + 8, :] for s in range(slabs)]
    sub = lax.broadcasted_iota(jnp.int32, (8, n), 0)
    lane = lax.broadcasted_iota(jnp.int32, (8, n), 1)
    E = [(lane == sub + 8 * s).astype(F32) for s in range(slabs)]
    R = []
    for g in range(slabs):
        C = [[jnp.broadcast_to(D[s][:, 8 * g + k : 8 * g + k + 1], (8, n)) for s in range(g, slabs)] for k in range(8)]
        scale = jnp.zeros((8, n), F32)
        M = []
        for j in range(8):
            piv = jnp.broadcast_to(C[j][0][j : j + 1, :], (8, n))
            inv = 1.0 / piv
            root = lax.rsqrt(piv)
            root = root * (1.5 - 0.5 * piv * root * root)
            scale = jnp.where(sub == j, root, scale)
            M.append([C[j][t] * inv if t else jnp.where(sub > j, C[j][t] * inv, 0.0) for t in range(slabs - g)])
            for k in range(j + 1, 8):
                top = jnp.broadcast_to(C[k][0][j : j + 1, :], (8, n))
                for t in range(slabs - g):
                    C[k][t] = C[k][t] - M[j][t] * top
        for j in range(8):
            dj = jnp.broadcast_to(D[g][j : j + 1, :], (8, n))
            ej = jnp.broadcast_to(E[g][j : j + 1, :], (8, n))
            for t in range(slabs - g):
                D[g + t] = D[g + t] - M[j][t] * dj
                E[g + t] = E[g + t] - M[j][t] * ej
        R.append(jnp.where(lane >= sub + 8 * g, D[g] * scale, 0.0))
        E[g] = E[g] * scale
    return jnp.concatenate(R, axis=0), jnp.concatenate(E, axis=0)


def first_half(gram, r, x00):
    rr, xx = factor_block(gram[:128, :128])
    r[:, :128] = rr
    x00[...] = xx
    r[:, 128:] = dot(xx, gram[:128, 128:])


def second_half(gram, r0, x00, r, x):
    r01 = r0[:, 128:]
    r[:128, :] = r0[...]
    r[128:, :128] = jnp.zeros((128, 128), F32)
    x[:128, :128] = x00[...]
    x[:128, 128:] = jnp.zeros((128, 128), F32)
    r01t = r01.T
    left = dot(r01t, x00[...])
    s = gram[128:, 128:] - dot(r01t, r01)
    rr, xx = factor_block(s)
    r[128:, 128:] = rr
    x[128:, 128:] = xx
    x[128:, :128] = -dot(xx, left)


def factor(gram):
    half = jax.ShapeDtypeStruct((128, 256), F32)
    block = jax.ShapeDtypeStruct((128, 128), F32)
    whole = jax.ShapeDtypeStruct((256, 256), F32)
    r0, x00 = pl.pallas_call(first_half, out_shape=(half, block), name="factor_a")(gram)
    return pl.pallas_call(second_half, out_shape=(whole, whole), name="factor_b")(gram, r0, x00)


def mine_and_other(a, core):
    top, low = a[:128], a[128:]
    return jnp.where(core == 0, top, low), jnp.where(core == 0, low, top)


def sum_over_cores(a, core):
    mine, other = mine_and_other(a, core)
    return mine + lax.ppermute(other, "rows", CORE_SWAP)


def both_halves(a, core):
    other = lax.ppermute(a, "rows", CORE_SWAP)
    return jnp.concatenate([jnp.where(core == 0, a, other), jnp.where(core == 0, other, a)], axis=0)


def to_pieces(a):
    n = a.shape[1]
    h = n // 32
    return a.reshape(32 // h, h, n // 128, 128).transpose(0, 2, 1, 3).reshape(8, h, 128)


def from_pieces(a):
    h = a.shape[1]
    n = 32 * h
    return a.reshape(32 // h, n // 128, h, 128).transpose(0, 2, 1, 3).reshape(32, n)


def scatter_sum(a, core):
    n = a.shape[1]
    a = sum_over_cores(a, core)
    a = exchange(a.reshape(4, 32, n), "rows", GROUP_Y).sum(0)
    return exchange(to_pieces(a), "rows", GROUP_Z).sum(0)


def gather_back(a, core):
    a = from_pieces(exchange(copies(a, 8), "rows", GROUP_Z))
    a = exchange(copies(a, 4), "rows", GROUP_Y)
    return both_halves(a.reshape(128, a.shape[2]), core)


def shards(panel, trailing):
    x = lax.axis_index("cols")
    core = lax.axis_index("rows") % 2
    below = lax.ppermute(panel, "cols", X_UP)
    above = lax.ppermute(panel, "cols", X_DOWN)
    far_a = lax.ppermute(below[:256], "cols", X_UP)
    far_b = lax.ppermute(above[256:], "cols", X_DOWN)

    gram = dot(panel, panel, ((0,), (0,)))
    g = scatter_sum(gram, core)
    g = exchange(copies(g, 4), "cols").sum(0)
    gram = gather_back(g, core)
    rfactor, inverse = factor(gram)

    far = jnp.concatenate([far_a, far_b], axis=0)
    pieces = (panel, below, above, far)
    places = (x, (x + 3) % 4, (x + 1) % 4, (x + 2) % 4)
    cross = 0.0
    block = jnp.zeros((2048, 256), F32)
    for piece, q in zip(pieces, places):
        rows = lax.dynamic_slice(trailing, (q * 512, 0), (512, 512))
        cross = cross + dot(piece, rows, ((0,), (0,)))
        block = lax.dynamic_update_slice(block, piece, (q * 512, 0))
    cross = gather_back(scatter_sum(cross, core), core)

    projected = dot(inverse, cross)
    weights = dot(inverse, projected, ((0,), (0,)))
    updated = trailing - dot(block, weights)
    return rfactor, projected, updated


def solution(mesh):
    placed = (P(("rows", "cols"), None), P("rows", "cols"))
    return jax.shard_map(
        shards,
        mesh=mesh,
        in_specs=placed,
        out_specs=(P(), P(None, "cols"), P("rows", "cols")),
        check_vma=False,
    )
```

time: 314 us -> 154 us (0.49)
  waiting for transfers between devices: 187 us -> 28.6 us
  starting transfers between devices: 0.04 us -> 52.6 us
  other arithmetic: 55 us -> 2.6 us
  between operations: 15.6 us -> 0.96 us
  Pallas kernels: 0 us -> 12.1 us
  blocking collectives: 30 us -> 34.3 us
    psum x1 -> x0, waiting for transfers between devices: 187 us -> none  [in_one(): running = lax.psum(jnp.concatenate([a.ravel() for a in arrays]), axis)]
    another operation x10 -> x0, other arithmetic: 54 us -> none  [the longest x6 34.1 us: shards(): rfactor = jnp.linalg.cholesky(gram).T]
    ppermute x0 -> x8, starting transfers between devices: none -> 31.6 us  [the longest x2 18.1 us: both_halves(): other = lax.ppermute(a, 'rows', CORE_SWAP)]
    all_to_all x0 -> x6, waiting for transfers between devices: none -> 24.8 us  [exchange(): return lax.all_to_all(a, axis, 0, 0, axis_index_groups=groups, tiled=True)]
    all_to_all x0 -> x6, starting transfers between devices: none -> 21 us  [exchange(): return lax.all_to_all(a, axis, 0, 0, axis_index_groups=groups, tiled=True)]
    pallas_call x0 -> x2, Pallas kernels: none -> 12.1 us  [the longest x1 6.33 us: factor(): pl.pallas_call(second_half, out_shape=(whole, whole), name='factor_b')]
    another operation x8 -> x0, matrix products: 5.65 us -> none  [the longest x6 5.18 us: lower_solve(): return jax.scipy.linalg.solve_triangular(rfactor.T, right, lower=True)]
    another operation x12 -> x0, local copies, waits for them, and re-layouts: 5.29 us -> none
  transfers between devices with their start and end apart: 1 -> 14, of which waited for: 1 -> 8; matrix products, arithmetic and copies ran while one was open for 0% -> 9% of each run, Pallas kernels for 0% -> 8%
where the time goes in v1:
time: 154 us
  starting transfers between devices  52.6 us (34%)
  blocking collectives  34.3 us (22%)
  waiting for transfers between devices  28.6 us (19%)
  matrix products  17.6 us (11%)
  Pallas kernels  12.1 us (8%)
  local copies, waits for them, and re-layouts  4.76 us (3%)
  other arithmetic  2.6 us (2%)
    all_to_all x3, blocking collectives, exchange(): return lax.all_to_all(a, axis, 0, 0, axis_index_groups=groups, tiled=True)  34.3 us
    all_to_all x6, waiting for transfers between devices, exchange(): return lax.all_to_all(a, axis, 0, 0, axis_index_groups=groups, tiled=True)  24.8 us
    all_to_all x6, starting transfers between devices, exchange(): return lax.all_to_all(a, axis, 0, 0, axis_index_groups=groups, tiled=True)  21 us
    ppermute x2, starting transfers between devices, both_halves(): other = lax.ppermute(a, 'rows', CORE_SWAP)  18.1 us
    dot_general x8, matrix products, dot(): lax.dot_general(a, b, (dims, ((), ())), precision=precision, preferred_el...  17.6 us
    ppermute x2, starting transfers between devices, sum_over_cores(): return mine + lax.ppermute(other, 'rows', CORE_SWAP)  6.47 us
    pallas_call x1, Pallas kernels, factor(): pl.pallas_call(second_half, out_shape=(whole, whole), name='factor_b')  6.33 us
    pallas_call x1, Pallas kernels, factor(): pl.pallas_call(first_half, out_shape=(half, block), name='factor_a')(gram)  5.79 us
  transfers between devices with their start and end apart: 14, of which 8 were waited for; matrix products, arithmetic and copies ran while one was open for 9% of the time, Pallas kernels for 8%

profile of v1, /device:TPU:1, one launch (start us, length us, event | category | flops | bytes accessed | tf_op | source)
XLA Modules:
  0.0 153.6 jit_solution(10270482882716380905)
XLA Ops:
  0.6 0.0 copy-start.2
  0.6 2.1 %collective-permute-start.2 = (f32[512,256]{1,0:T(8,128)}, f32[512,256]{1,0:T(8,128)S(1)}, u32[]{:S(2)}, u32[]{:S(2)}) collective-permute-start(f32[512,256]{1,0:T(8,128)} %param.2), channel_id=1, source_target_pairs={{0,1},{1,2},{2,3},{3,0},{4,5},{5,6},{6,7},{7,4},{8,9},{9,10},{10,1... | collective-permute-start | bytes 1572872 | tf_op jit(solution)/shard_map/ppermute | solution.py:143
  2.7 1.4 collective-permute-start.3
  4.1 2.2 %fusion.17 = f32[256,256]{1,0:T(8,128)S(1)} fusion(f32[512,256]{1,0:T(8,128)} %param.2), kind=kOutput, calls=%fused_computation.36 | convolution fusion | flops 402653184 | bytes 786432 | tf_op jit(solution)/shard_map/dot_general | solution.py:25
  6.4 3.1 %collective-permute-start = (f32[128,256]{1,0:T(8,128)S(1)}, f32[128,256]{1,0:T(8,128)S(1)}, u32[]{:S(2)}, u32[]{:S(2)}) collective-permute-start(f32[128,256]{1,0:T(8,128)S(1)} %slice_select_fusion.1), channel_id=1, source_target_pairs={{0,4},{4,0},{8,12},{12,8},{16,20},{20,16},{24,28},{28,24},{32,36},... | collective-permute-start | bytes 393224 | tf_op jit(solution)/shard_map/ppermute | solution.py:107
  9.5 0.0 copy-done.2
  9.5 2.3 %fusion.6 = f32[512,256]{0,1:T(8,128)S(1)} fusion(f32[512,256]{1,0:T(8,128)S(1)} %copy-done.2, f32[2048,512]{1,0:T(8,128)} %param.3, s32[]{:T(128)S(6)} %select_n.82), kind=kOutput, calls=%fused_computation.9 | convolution fusion | flops 805306368 | bytes 2097156 | tf_op jit(solution)/shard_map/dot_general | solution.py:25
  11.8 1.8 %collective-permute-done.2 = f32[512,256]{1,0:T(8,128)S(1)} collective-permute-done((f32[512,256]{1,0:T(8,128)}, f32[512,256]{1,0:T(8,128)S(1)}, u32[]{:S(2)}, u32[]{:S(2)}) %collective-permute-start.2) | collective-permute-done | bytes 524320 | tf_op jit(solution)/shard_map/ppermute | solution.py:143
  13.7 0.0 copy-start.3
  13.7 0.0 copy-start
  13.7 1.9 %collective-permute-start.4 = (f32[256,256]{1,0:T(8,128)S(1)}, f32[256,256]{1,0:T(8,128)S(1)}, u32[]{:S(2)}, u32[]{:S(2)}) collective-permute-start(f32[256,256]{1,0:T(8,128)S(1)} %slice.26), channel_id=1, source_target_pairs={{0,1},{1,2},{2,3},{3,0},{4,5},{5,6},{6,7},{7,4},{8,9},{9,10},{10,1... | collective-permute-start | bytes 786440 | tf_op jit(solution)/shard_map/ppermute | solution.py:145
  15.7 0.0 collective-permute-done.3
  15.7 1.6 %collective-permute-start.5 = (f32[256,256]{1,0:T(8,128)S(1)}, f32[256,256]{1,0:T(8,128)S(1)}, u32[]{:S(2)}, u32[]{:S(2)}) collective-permute-start(f32[256,256]{1,0:T(8,128)S(1)} %slice.27), channel_id=1, source_target_pairs={{0,3},{1,0},{2,1},{3,2},{4,7},{5,4},{6,5},{7,6},{8,11},{9,8},{10,9... | collective-permute-start | bytes 786440 | tf_op jit(solution)/shard_map/ppermute | solution.py:146
  17.3 2.3 %convolution_add_fusion.1 = f32[512,256]{0,1:T(8,128)S(1)} fusion(f32[512,256]{0,1:T(8,128)S(1)} %fusion.6, f32[512,256]{1,0:T(8,128)S(1)} %collective-permute-done.2, f32[2048,512]{1,0:T(8,128)} %param.3, s32[]{:T(128)S(6)} %select_n.84), kind=kOutput, calls=%fused_computation.3 | convolution fusion | flops 805437440 | bytes 2621444 | tf_op jit(solution)/shard_map/dot_general | solution.py:25
  19.6 0.0 copy-done.3
  19.6 1.3 collective-permute-done.4
  20.9 0.7 collective-permute-done.5
  21.6 0.0 copy-done
  21.6 1.1 fusion.2
  22.7 0.0 copy-done.4
  22.7 1.1 fusion.1
  23.9 3.3 %collective-permute-start.6 = (f32[128,512]{1,0:T(8,128)S(1)}, f32[128,512]{1,0:T(8,128)S(1)}, u32[]{:S(2)}, u32[]{:S(2)}) collective-permute-start(f32[128,512]{1,0:T(8,128)S(1)} %slice_select_fusion), channel_id=1, source_target_pairs={{0,4},{4,0},{8,12},{12,8},{16,20},{20,16},{24,28},{28,24},{32,36},... | collective-permute-start | bytes 786440 | tf_op jit(solution)/shard_map/ppermute | solution.py:107
  27.2 0.0 collective-permute-done
  27.2 9.8 %all_to_all.45 = f32[4,32,256]{2,1,0:T(8,128)S(1)} all-to-all(f32[4,32,256]{2,1,0:T(8,128)S(1)} %bitcast.45), channel_id=1, replica_groups={{0,64,128,192},{4,68,132,196},{8,72,136,200},{12,76,140,204},{16,80,144..., dimensions={0} | all-to-all | bytes 262144 | tf_op jit(solution)/shard_map/all_to_all | solution.py:29
  37.1 14.9 %all_to_all.46 = f32[8,8,128]{2,1,0:T(8,128)S(1)} all-to-all(f32[8,8,128]{2,1,0:T(8,128)S(1)} %bitcast.52), channel_id=1, replica_groups={{0,8,16,24,32,40,48,56},{4,12,20,28,36,44,52,60},{64,72,80,88,96,104,11..., dimensions={0} | all-to-all | bytes 65536 | tf_op jit(solution)/shard_map/all_to_all | solution.py:29
  52.0 0.6 broadcast_in_dim.16
  52.6 4.0 %all-to-all-start.2 = ((f32[4,8,128]{2,1,0:T(8,128)}), f32[4,8,128]{2,1,0:T(8,128)S(1)}, u32[]{:S(2)}, u32[]{:S(2)}) async-start(f32[4,8,128]{2,1,0:T(8,128)} %broadcast_in_dim.16), calls=%async_computation.2 | async-start | bytes 32768 | tf_op jit(solution)/shard_map/all_to_all | solution.py:29
  56.6 0.0 collective-permute-done.6
  56.6 0.8 select_add_fusion
  57.3 3.5 %all-to-all-done.2 = f32[4,8,128]{2,1,0:T(8,128)S(1)} async-done(((f32[4,8,128]{2,1,0:T(8,128)}), f32[4,8,128]{2,1,0:T(8,128)S(1)}, u32[]{:S(2)}, u32[]{:S(2)}) %all-to-all-start.2) | async-done | bytes 16416 | tf_op jit(solution)/shard_map/all_to_all | solution.py:29
  60.8 3.4 %all-to-all-start.5 = ((f32[4,32,512]{2,1,0:T(8,128)}), f32[4,32,512]{2,1,0:T(8,128)S(1)}, u32[]{:S(2)}, u32[]{:S(2)}) async-start(f32[4,32,512]{2,1,0:T(8,128)} %bitcast.9), calls=%async_computation.5 | async-start | bytes 524288 | tf_op jit(solution)/shard_map/all_to_all | solution.py:29
  64.2 5.5 %all-to-all-done.5 = f32[4,32,512]{2,1,0:T(8,128)S(1)} async-done(((f32[4,32,512]{2,1,0:T(8,128)}), f32[4,32,512]{2,1,0:T(8,128)S(1)}, u32[]{:S(2)}, u32[]{:S(2)}) %all-to-all-start.5) | async-done | bytes 262176 | tf_op jit(solution)/shard_map/all_to_all | solution.py:29
  69.7 0.6 broadcast_in_dim.17
  70.3 3.3 %all-to-all-start.3 = ((f32[8,8,128]{2,1,0:T(8,128)}), f32[8,8,128]{2,1,0:T(8,128)S(1)}, u32[]{:S(2)}, u32[]{:S(2)}) async-start(f32[8,8,128]{2,1,0:T(8,128)} %broadcast_in_dim.17), calls=%async_computation.3 | async-start | bytes 65536 | tf_op jit(solution)/shard_map/all_to_all | solution.py:29
  73.7 6.7 %all-to-all-done.3 = f32[8,8,128]{2,1,0:T(8,128)S(1)} async-done(((f32[8,8,128]{2,1,0:T(8,128)}), f32[8,8,128]{2,1,0:T(8,128)S(1)}, u32[]{:S(2)}, u32[]{:S(2)}) %all-to-all-start.3) | async-done | bytes 32800 | tf_op jit(solution)/shard_map/all_to_all | solution.py:29
  80.5 9.6 %all_to_all.47 = f32[8,16,128]{2,1,0:T(8,128)S(1)} all-to-all(f32[8,16,128]{2,1,0:T(8,128)S(1)} %bitcast.48), channel_id=1, replica_groups={{0,8,16,24,32,40,48,56},{4,12,20,28,36,44,52,60},{64,72,80,88,96,104,11..., dimensions={0} | all-to-all | bytes 131072 | tf_op jit(solution)/shard_map/all_to_all | solution.py:29
  90.1 0.7 broadcast_in_dim.38
  90.7 3.3 %all-to-all-start.4 = ((f32[4,32,256]{2,1,0:T(8,128)}), f32[4,32,256]{2,1,0:T(8,128)S(1)}, u32[]{:S(2)}, u32[]{:S(2)}) async-start(f32[4,32,256]{2,1,0:T(8,128)} %broadcast_in_dim.38), calls=%async_computation.4 | async-start | bytes 262144 | tf_op jit(solution)/shard_map/all_to_all | solution.py:29
  94.1 4.8 %all-to-all-done.4 = f32[4,32,256]{2,1,0:T(8,128)S(1)} async-done(((f32[4,32,256]{2,1,0:T(8,128)}), f32[4,32,256]{2,1,0:T(8,128)S(1)}, u32[]{:S(2)}, u32[]{:S(2)}) %all-to-all-start.4) | async-done | bytes 131104 | tf_op jit(solution)/shard_map/all_to_all | solution.py:29
  98.8 0.6 broadcast_in_dim.39
  99.5 3.4 %all-to-all-start.7 = ((f32[8,16,128]{2,1,0:T(8,128)}), f32[8,16,128]{2,1,0:T(8,128)S(1)}, u32[]{:S(2)}, u32[]{:S(2)}) async-start(f32[8,16,128]{2,1,0:T(8,128)} %broadcast_in_dim.39), calls=%async_computation.7 | async-start | bytes 131072 | tf_op jit(solution)/shard_map/all_to_all | solution.py:29
  102.8 0.1 broadcast_in_dim.42
  103.0 0.0 copy-start.5
  103.0 9.0 %collective-permute-start.1 = (f32[128,256]{1,0:T(8,128)S(1)}, f32[128,256]{1,0:T(8,128)}, u32[]{:S(2)}, u32[]{:S(2)}) collective-permute-start(f32[128,256]{1,0:T(8,128)S(1)} %bitcast.44), channel_id=1, source_target_pairs={{0,4},{4,0},{8,12},{12,8},{16,20},{20,16},{24,28},{28,24},{32,36},... | collective-permute-start | bytes 393224 | tf_op jit(solution)/shard_map/ppermute | solution.py:111
  112.0 0.0 all-to-all-done.7
  112.1 0.7 broadcast_in_dim.41
  112.8 3.6 %all-to-all-start.8 = ((f32[4,32,512]{2,1,0:T(8,128)}), f32[4,32,512]{2,1,0:T(8,128)S(1)}, u32[]{:S(2)}, u32[]{:S(2)}) async-start(f32[4,32,512]{2,1,0:T(8,128)} %broadcast_in_dim.41), calls=%async_computation.8 | async-start | bytes 524288 | tf_op jit(solution)/shard_map/all_to_all | solution.py:29
  116.4 1.1 constant_dynamic-update-slice_fusion.4
  117.5 0.0 copy-done.5
  117.5 4.3 %all-to-all-done.8 = f32[4,32,512]{2,1,0:T(8,128)S(1)} async-done(((f32[4,32,512]{2,1,0:T(8,128)}), f32[4,32,512]{2,1,0:T(8,128)S(1)}, u32[]{:S(2)}, u32[]{:S(2)}) %all-to-all-start.8) | async-done | bytes 262176 | tf_op jit(solution)/shard_map/all_to_all | solution.py:29
  121.9 9.1 %collective-permute-start.7 = (f32[128,512]{1,0:T(8,128)S(1)}, f32[128,512]{1,0:T(8,128)S(1)}, u32[]{:S(2)}, u32[]{:S(2)}) collective-permute-start(f32[128,512]{1,0:T(8,128)S(1)} %bitcast.43), channel_id=1, source_target_pairs={{0,4},{4,0},{8,12},{12,8},{16,20},{20,16},{24,28},{28,24},{32,36},... | collective-permute-start | bytes 786440 | tf_op jit(solution)/shard_map/ppermute | solution.py:111
  131.0 0.0 collective-permute-done.1
  131.0 0.9 broadcast_select_fusion.3
  132.0 0.7 pad_maximum_fusion.gram
  132.7 5.8 %factor_a.1 = (f32[128,256]{1,0:T(8,128)}, f32[128,128]{1,0:T(8,128)}) custom-call(f32[256,256]{1,0:T(8,128)} %pad_maximum_fusion.gram), custom_call_target="tpu_custom_call" | custom-call | tf_op jit(solution)/shard_map/factor_a/pallas_call | solution.py:96
  138.5 6.3 %factor_b.1 = (f32[256,256]{1,0:T(8,128)}, f32[256,256]{1,0:T(8,128)}) custom-call(f32[256,256]{1,0:T(8,128)} %pad_maximum_fusion.gram, f32[128,256]{1,0:T(8,128)} %get-tuple-element.7.r0, f32[128,128]{1,0:T(8,128)} %get-tuple-element.8.x00), custom_call_target="tpu_custom_call" | custom-call | tf_op jit(solution)/shard_map/factor_b/pallas_call | solution.py:97
  144.9 0.0 collective-permute-done.7
  144.9 0.1 broadcast_select_fusion.1
  144.9 1.7 %fusion.8 = f32[256,512]{1,0:T(8,128)S(1)} fusion(f32[256,256]{1,0:T(8,128)} %get-tuple-element.10, f32[128,512]{1,0:T(8,128)S(1)} %get-tuple-element.12, f32[128,512]{1,0:T(8,128)S(1)} %get-tuple-element.11), kind=kOutput, calls=%fused_computation.11 | convolution fusion | flops 402784256 | bytes 1310720 | tf_op jit(solution)/shard_map/dot_general | solution.py:25
  146.7 0.0 copy-start.6
  146.7 1.8 %fusion.18 = f32[256,512]{1,0:T(8,128)S(1)} fusion(f32[256,256]{1,0:T(8,128)} %get-tuple-element.10, f32[256,512]{1,0:T(8,128)S(1)} %fusion.8), kind=kOutput, calls=%fused_computation.37 | convolution fusion | flops 402653184 | bytes 1310720 | tf_op jit(solution)/shard_map/dot_general | solution.py:25
  148.4 0.0 copy-done.1
  148.5 5.1 %convolution_subtract_fusion = f32[2048,512]{1,0:T(8,128)} fusion(f32[2048,512]{1,0:T(8,128)S(1)} %copy-done.1, f32[2048,256]{1,0:T(8,128)S(1)} %constant_dynamic-update-slice_fusion.2, f32[256,512]{1,0:T(8,128)S(1)} %fusion.18), kind=kOutput, calls=%fused_computation | convolution fusion | flops 3222274048 | bytes 11010048 | tf_op jit(solution)/shard_map/dot_general | solution.py:25
  153.6 0.0 copy-done.6
  (21 shorter events, 0.4 us)
Async XLA Ops:
  0.6 8.9 %copy-start.2 = (f32[512,256]{1,0:T(8,128)S(1)}, f32[512,256]{1,0:T(8,128)}, u32[]{:S(2)}) copy-start(f32[512,256]{1,0:T(8,128)} %param.2) | copy-start | bytes 1572868
  0.6 13.0 %collective-permute-start.2 = (f32[512,256]{1,0:T(8,128)}, f32[512,256]{1,0:T(8,128)S(1)}, u32[]{:S(2)}, u32[]{:S(2)}) collective-permute-start(f32[512,256]{1,0:T(8,128)} %param.2), channel_id=1, source_target_pairs={{0,1},{1,2},{2,3},{3,0},{4,5},{5,6},{6,7},{7,4},{8,9},{9,10},{10,1... | collective-permute-start | bytes 1572872 | tf_op jit(solution)/shard_map/ppermute | solution.py:143
  2.7 12.9 %collective-permute-start.3 = (f32[512,256]{1,0:T(8,128)}, f32[512,256]{1,0:T(8,128)S(1)}, u32[]{:S(2)}, u32[]{:S(2)}) collective-permute-start(f32[512,256]{1,0:T(8,128)} %param.2), channel_id=1, source_target_pairs={{0,3},{1,0},{2,1},{3,2},{4,7},{5,4},{6,5},{7,6},{8,11},{9,8},{10,9... | collective-permute-start | bytes 1572872 | tf_op jit(solution)/shard_map/ppermute | solution.py:144
  6.4 20.9 %collective-permute-start = (f32[128,256]{1,0:T(8,128)S(1)}, f32[128,256]{1,0:T(8,128)S(1)}, u32[]{:S(2)}, u32[]{:S(2)}) collective-permute-start(f32[128,256]{1,0:T(8,128)S(1)} %slice_select_fusion.1), channel_id=1, source_target_pairs={{0,4},{4,0},{8,12},{12,8},{16,20},{20,16},{24,28},{28,24},{32,36},... | collective-permute-start | bytes 393224 | tf_op jit(solution)/shard_map/ppermute | solution.py:107
  13.7 6.0 %copy-start.3 = (f32[512,256]{1,0:T(8,128)}, f32[512,256]{1,0:T(8,128)S(1)}, u32[]{:S(2)}) copy-start(f32[512,256]{1,0:T(8,128)S(1)} %collective-permute-done.2) | copy-start | bytes 1572868
  13.7 7.9 %copy-start = (f32[2048,512]{1,0:T(8,128)S(1)}, f32[2048,512]{1,0:T(8,128)}, u32[]{:S(2)}) copy-start(f32[2048,512]{1,0:T(8,128)} %param.3) | copy-start | bytes 12582916
  13.7 7.2 %collective-permute-start.4 = (f32[256,256]{1,0:T(8,128)S(1)}, f32[256,256]{1,0:T(8,128)S(1)}, u32[]{:S(2)}, u32[]{:S(2)}) collective-permute-start(f32[256,256]{1,0:T(8,128)S(1)} %slice.26), channel_id=1, source_target_pairs={{0,1},{1,2},{2,3},{3,0},{4,5},{5,6},{6,7},{7,4},{8,9},{9,10},{10,1... | collective-permute-start | bytes 786440 | tf_op jit(solution)/shard_map/ppermute | solution.py:145
  15.7 7.0 %copy-start.4 = (f32[512,256]{1,0:T(8,128)}, f32[512,256]{1,0:T(8,128)S(1)}, u32[]{:S(2)}) copy-start(f32[512,256]{1,0:T(8,128)S(1)} %collective-permute-done.3) | copy-start | bytes 1572868
  15.7 5.9 %collective-permute-start.5 = (f32[256,256]{1,0:T(8,128)S(1)}, f32[256,256]{1,0:T(8,128)S(1)}, u32[]{:S(2)}, u32[]{:S(2)}) collective-permute-start(f32[256,256]{1,0:T(8,128)S(1)} %slice.27), channel_id=1, source_target_pairs={{0,3},{1,0},{2,1},{3,2},{4,7},{5,4},{6,5},{7,6},{8,11},{9,8},{10,9... | collective-permute-start | bytes 786440 | tf_op jit(solution)/shard_map/ppermute | solution.py:146
  23.9 32.7 %collective-permute-start.6 = (f32[128,512]{1,0:T(8,128)S(1)}, f32[128,512]{1,0:T(8,128)S(1)}, u32[]{:S(2)}, u32[]{:S(2)}) collective-permute-start(f32[128,512]{1,0:T(8,128)S(1)} %slice_select_fusion), channel_id=1, source_target_pairs={{0,4},{4,0},{8,12},{12,8},{16,20},{20,16},{24,28},{28,24},{32,36},... | collective-permute-start | bytes 786440 | tf_op jit(solution)/shard_map/ppermute | solution.py:107
  52.6 8.2 %all-to-all-start.2 = ((f32[4,8,128]{2,1,0:T(8,128)}), f32[4,8,128]{2,1,0:T(8,128)S(1)}, u32[]{:S(2)}, u32[]{:S(2)}) async-start(f32[4,8,128]{2,1,0:T(8,128)} %broadcast_in_dim.16), calls=%async_computation.2 | async-start | bytes 32768 | tf_op jit(solution)/shard_map/all_to_all | solution.py:29
  60.8 8.9 %all-to-all-start.5 = ((f32[4,32,512]{2,1,0:T(8,128)}), f32[4,32,512]{2,1,0:T(8,128)S(1)}, u32[]{:S(2)}, u32[]{:S(2)}) async-start(f32[4,32,512]{2,1,0:T(8,128)} %bitcast.9), calls=%async_computation.5 | async-start | bytes 524288 | tf_op jit(solution)/shard_map/all_to_all | solution.py:29
  70.3 10.1 %all-to-all-start.3 = ((f32[8,8,128]{2,1,0:T(8,128)}), f32[8,8,128]{2,1,0:T(8,128)S(1)}, u32[]{:S(2)}, u32[]{:S(2)}) async-start(f32[8,8,128]{2,1,0:T(8,128)} %broadcast_in_dim.17), calls=%async_computation.3 | async-start | bytes 65536 | tf_op jit(solution)/shard_map/all_to_all | solution.py:29
  90.7 8.1 %all-to-all-start.4 = ((f32[4,32,256]{2,1,0:T(8,128)}), f32[4,32,256]{2,1,0:T(8,128)S(1)}, u32[]{:S(2)}, u32[]{:S(2)}) async-start(f32[4,32,256]{2,1,0:T(8,128)} %broadcast_in_dim.38), calls=%async_computation.4 | async-start | bytes 262144 | tf_op jit(solution)/shard_map/all_to_all | solution.py:29
  99.5 12.5 %all-to-all-start.7 = ((f32[8,16,128]{2,1,0:T(8,128)}), f32[8,16,128]{2,1,0:T(8,128)S(1)}, u32[]{:S(2)}, u32[]{:S(2)}) async-start(f32[8,16,128]{2,1,0:T(8,128)} %broadcast_in_dim.39), calls=%async_computation.7 | async-start | bytes 131072 | tf_op jit(solution)/shard_map/all_to_all | solution.py:29
  103.0 14.5 %copy-start.5 = (f32[512,256]{1,0:T(8,128)S(1)}, f32[512,256]{1,0:T(8,128)}, u32[]{:S(2)}) copy-start(f32[512,256]{1,0:T(8,128)} %copy-done.4) | copy-start | bytes 1572868
  103.0 28.0 %collective-permute-start.1 = (f32[128,256]{1,0:T(8,128)S(1)}, f32[128,256]{1,0:T(8,128)}, u32[]{:S(2)}, u32[]{:S(2)}) collective-permute-start(f32[128,256]{1,0:T(8,128)S(1)} %bitcast.44), channel_id=1, source_target_pairs={{0,4},{4,0},{8,12},{12,8},{16,20},{20,16},{24,28},{28,24},{32,36},... | collective-permute-start | bytes 393224 | tf_op jit(solution)/shard_map/ppermute | solution.py:111
  112.8 9.1 %all-to-all-start.8 = ((f32[4,32,512]{2,1,0:T(8,128)}), f32[4,32,512]{2,1,0:T(8,128)S(1)}, u32[]{:S(2)}, u32[]{:S(2)}) async-start(f32[4,32,512]{2,1,0:T(8,128)} %broadcast_in_dim.41), calls=%async_computation.8 | async-start | bytes 524288 | tf_op jit(solution)/shard_map/all_to_all | solution.py:29
  121.9 23.0 %collective-permute-start.7 = (f32[128,512]{1,0:T(8,128)S(1)}, f32[128,512]{1,0:T(8,128)S(1)}, u32[]{:S(2)}, u32[]{:S(2)}) collective-permute-start(f32[128,512]{1,0:T(8,128)S(1)} %bitcast.43), channel_id=1, source_target_pairs={{0,4},{4,0},{8,12},{12,8},{16,20},{20,16},{24,28},{28,24},{32,36},... | collective-permute-start | bytes 786440 | tf_op jit(solution)/shard_map/ppermute | solution.py:111
  144.8 3.6 %copy-start.1 = (f32[2048,512]{1,0:T(8,128)S(1)}, f32[2048,512]{1,0:T(8,128)}, u32[]{:S(2)}) copy-start(f32[2048,512]{1,0:T(8,128)} %param.3) | copy-start | bytes 12582916
  146.7 6.9 %copy-start.6 = (f32[256,512]{1,0:T(8,128)}, f32[256,512]{1,0:T(8,128)S(1)}, u32[]{:S(2)}) copy-start(f32[256,512]{1,0:T(8,128)S(1)} %fusion.8) | copy-start | bytes 1572868

commit v2 on v1

v2 whole, which is shorter than its diff:
```python
import jax
import jax.numpy as jnp
from jax import lax
from jax.experimental import pallas as pl
from jax.experimental.pallas import tpu as pltpu
from jax.sharding import PartitionSpec as P

NY, NZ, NC, NX = 4, 8, 2, 4
HIGHEST = lax.Precision.HIGHEST
F32 = jnp.float32


def row_id(y, z, c):
    return (y * NZ + z) * NC + c


GROUP_YZ = [[row_id(y, z, c) for y in range(NY) for z in range(NZ)] for c in range(NC)]
CORE_SWAP = [(i, i ^ 1) for i in range(NY * NZ * NC)]
X_UP = [(i, (i + 1) % NX) for i in range(NX)]
X_DOWN = [(i, (i - 1) % NX) for i in range(NX)]


def dot(a, b, dims=((1,), (0,)), precision=HIGHEST):
    return lax.dot_general(a, b, (dims, ((), ())), precision=precision, preferred_element_type=F32)


def exchange(a, axis, groups=None):
    return lax.all_to_all(a, axis, 0, 0, axis_index_groups=groups, tiled=True)


def split(a):
    hi = a.astype(jnp.bfloat16)
    return hi, (a - hi.astype(F32)).astype(jnp.bfloat16)


def product(a, b):
    (ah, al), (bh, bl) = a, b
    return dot(ah, bh, precision=None) + (dot(ah, bl, precision=None) + dot(al, bh, precision=None))


def copies(a, n):
    return jnp.broadcast_to(a[None], (n, *a.shape))


def factor_block(d):
    n = 128
    slabs = n // 8
    D = [d[8 * s : 8 * s + 8, :] for s in range(slabs)]
    sub = lax.broadcasted_iota(jnp.int32, (8, n), 0)
    lane = lax.broadcasted_iota(jnp.int32, (8, n), 1)
    E = [(lane == sub + 8 * s).astype(F32) for s in range(slabs)]
    R = []
    for g in range(slabs):
        C = [[jnp.broadcast_to(D[s][:, 8 * g + k : 8 * g + k + 1], (8, n)) for s in range(g, slabs)] for k in range(8)]
        scale = jnp.zeros((8, n), F32)
        M = []
        for j in range(8):
            piv = jnp.broadcast_to(C[j][0][j : j + 1, :], (8, n))
            inv = 1.0 / piv
            root = lax.rsqrt(piv)
            root = root * (1.5 - 0.5 * piv * root * root)
            scale = jnp.where(sub == j, root, scale)
            M.append([C[j][t] * inv if t else jnp.where(sub > j, C[j][t] * inv, 0.0) for t in range(slabs - g)])
            for k in range(j + 1, 8):
                top = jnp.broadcast_to(C[k][0][j : j + 1, :], (8, n))
                for t in range(slabs - g):
                    C[k][t] = C[k][t] - M[j][t] * top
        for j in range(8):
            dj = jnp.broadcast_to(D[g][j : j + 1, :], (8, n))
            ej = jnp.broadcast_to(E[g][j : j + 1, :], (8, n))
            for t in range(slabs - g):
                D[g + t] = D[g + t] - M[j][t] * dj
                E[g + t] = E[g + t] - M[j][t] * ej
        R.append(jnp.where(lane >= sub + 8 * g, D[g] * scale, 0.0))
        E[g] = E[g] * scale
    return jnp.concatenate(R, axis=0), jnp.concatenate(E, axis=0)


def cut(src, start, out, first):
    across = src.shape[1] // 128
    h = 4 * across
    for p in range(32):
        r, c = divmod(p, across)
        out[p, first : first + h, :] = src[pl.ds(start + r * h, h), 128 * c : 128 * c + 128]


def paste(pieces, start, dst, first):
    across = dst.shape[1] // 128
    h = 4 * across
    for p in range(32):
        r, c = divmod(p, across)
        dst[pl.ds(start + r * h, h), 128 * c : 128 * c + 128] = pieces[p, first : first + h, :]


def starts(core):
    mine = pl.multiple_of(core[0] * 128, 128)
    return mine, pl.multiple_of(128 - mine, 128)


SMALL = pltpu.CompilerParams(vmem_limit_bytes=24 * 2**20)
SCALARS = pl.BlockSpec(memory_space=pltpu.SMEM)
VMEM = pl.BlockSpec(memory_space=pltpu.VMEM)


def shaped(*shape):
    return jax.ShapeDtypeStruct(shape, F32)


def first_half(core, mine, other, gram, r, x00):
    m, o = starts(core)
    paste(mine, m, gram, 16)
    paste(other, o, gram, 16)
    rr, xx = factor_block(gram[:128, :128])
    r[:, :128] = rr
    x00[...] = xx
    r[:, 128:] = dot(xx, gram[:128, 128:])


def second_half(gram, r0, x00, r, x):
    r01 = r0[:, 128:]
    r[:128, :] = r0[...]
    r[128:, :128] = jnp.zeros((128, 128), F32)
    x[:128, :128] = x00[...]
    x[:128, 128:] = jnp.zeros((128, 128), F32)
    r01t = r01.T
    left = dot(r01t, x00[...])
    s = gram[128:, 128:] - dot(r01t, r01)
    rr, xx = factor_block(s)
    r[128:, 128:] = rr
    x[128:, 128:] = xx
    x[128:, :128] = -dot(xx, left)


def factor(core, mine, other):
    gram, r0, x00 = pl.pallas_call(
        first_half,
        out_shape=(shaped(256, 256), shaped(128, 256), shaped(128, 128)),
        in_specs=[SCALARS, VMEM, VMEM],
        compiler_params=SMALL,
        name="factor_a",
    )(core, mine, other)
    return pl.pallas_call(
        second_half,
        out_shape=(shaped(256, 256), shaped(256, 256)),
        compiler_params=SMALL,
        name="factor_b",
    )(gram, r0, x00)


def accumulate(pieces, trails):
    cross, gram = 0.0, 0.0
    for piece, trail in zip(pieces, trails):
        flipped = piece.T
        cross = cross + product(split(flipped), split(trail))
        gram = gram + dot(flipped, piece)
    return cross, gram


def cross_own(places, panel, trail, cross, gram):
    cross[...], gram[...] = accumulate([panel[...]], [trail[...]])


def cross_near(places, b1, b2, a1, a2, cross0, gram0, tb, ta, cross, gram):
    c, g = accumulate([b1[...], b2[...], a1[...], a2[...]], [tb[:256, :], tb[256:, :], ta[:256, :], ta[256:, :]])
    cross[...] = cross0[...] + c
    gram[...] = gram0[...] + g


def cross_far(places, f1, f2, cross0, gram0, tf, mine, other, cross, gram):
    c, g = accumulate([f1[...], f2[...]], [tf[:256, :], tf[256:, :]])
    cross[...] = cross0[...] + c
    gram[...] = gram0[...] + g
    m, o = starts([places[4]])
    cut(cross, m, mine, 0)
    cut(gram, m, mine, 16)
    cut(cross, o, other, 0)
    cut(gram, o, other, 16)


def trail_at(k):
    return pl.BlockSpec((512, 512), lambda i, places: (places[k], 0))


def full(shape):
    return pl.BlockSpec(shape, lambda i, places: (0,) * len(shape))


def cross_call(kernel, name, places, arrays, trailing, which, outs, scratch=()):
    return pl.pallas_call(
        kernel,
        grid_spec=pltpu.PrefetchScalarGridSpec(
            num_scalar_prefetch=1,
            grid=(1,),
            in_specs=[full(a.shape) for a in arrays] + [trail_at(k) for k in which],
            out_specs=[full(o.shape) for o in outs],
            scratch_shapes=scratch,
        ),
        out_shape=outs,
        compiler_params=SMALL,
        name=name,
    )(places, *arrays, *[trailing] * len(which))


def finish(
    places, inverse, mine, other, own, b1, b2, a1, a2, f1, f2, trailing, projected, updated, cross, stage, result, reads, writes
):
    def read(k):
        rows = pl.ds(pl.multiple_of(places[k] * 512, 512), 512)
        return pltpu.make_async_copy(trailing.at[rows, :], stage.at[k], reads.at[k])

    def write(k):
        rows = pl.ds(pl.multiple_of(places[k] * 512, 512), 512)
        return pltpu.make_async_copy(result.at[k], updated.at[rows, :], writes.at[k])

    for k in range(4):
        read(k).start()
    m, o = starts([places[4]])
    paste(mine, m, cross, 0)
    paste(other, o, cross, 0)
    p = dot(inverse[...], cross[...])
    projected[...] = p
    w = split(dot(inverse[...], p, ((0,), (0,))))
    for k, parts in enumerate([(own,), (b1, b2), (a1, a2), (f1, f2)]):
        read(k).wait()
        n = 512 // len(parts)
        for i, part in enumerate(parts):
            rows = slice(n * i, n * i + n)
            result[k, rows, :] = stage[k, rows, :] - product(split(part[...]), w)
        write(k).start()
    for k in range(4):
        write(k).wait()


def finished(places, inverse, mine, other, pieces, trailing):
    return pl.pallas_call(
        finish,
        in_specs=[SCALARS] + [VMEM] * 10 + [pl.BlockSpec(memory_space=pltpu.HBM)],
        out_specs=[VMEM, pl.BlockSpec(memory_space=pltpu.HBM)],
        scratch_shapes=[pltpu.VMEM((256, 512), F32)]
        + [pltpu.VMEM((4, 512, 512), F32)] * 2
        + [pltpu.SemaphoreType.DMA((4,))] * 2,
        out_shape=(shaped(256, 512), shaped(2048, 512)),
        compiler_params=SMALL,
        name="finish",
    )(places, inverse, mine, other, *pieces, trailing)


def swap(a):
    return lax.ppermute(a, "rows", CORE_SWAP)


def shift(a, way):
    return lax.ppermute(a, "cols", way)


def shards(panel, trailing):
    x = lax.axis_index("cols")
    core = lax.axis_index("rows") % 2
    core_word = core.reshape(1)
    places = jnp.stack([x, (x + 3) % 4, (x + 1) % 4, (x + 2) % 4, core])

    top, low = panel[:256], panel[256:]
    b1 = shift(top, X_UP)
    a2 = shift(low, X_DOWN)
    b2 = shift(low, X_UP)
    a1 = shift(top, X_DOWN)

    f1 = shift(b1, X_UP)
    f2 = shift(a2, X_DOWN)
    sums = [shaped(256, 512), shaped(256, 256)]
    part = cross_call(cross_own, "cross_own", places, [panel], trailing, [0], sums)
    part = cross_call(cross_near, "cross_near", places, [b1, b2, a1, a2, *part], trailing, [1, 2], sums)
    halves = [shaped(32, 24, 128)] * 2
    scratch = [pltpu.VMEM((256, 512), F32), pltpu.VMEM((256, 256), F32)]
    mine, other = cross_call(cross_far, "cross_far", places, [f1, f2, *part], trailing, [3], halves, scratch)
    total = exchange(mine + swap(other), "rows", GROUP_YZ).sum(0)
    mine = exchange(copies(total, 32), "rows", GROUP_YZ)
    other = swap(mine)
    rfactor, inverse = factor(core_word, mine, other)
    projected, updated = finished(places, inverse, mine, other, (panel, b1, b2, a1, a2, f1, f2), trailing)
    return rfactor, projected, updated


def solution(mesh):
    placed = (P(("rows", "cols"), None), P("rows", "cols"))
    return jax.shard_map(
        shards,
        mesh=mesh,
        in_specs=placed,
        out_specs=(P(), P(None, "cols"), P("rows", "cols")),
        check_vma=False,
    )
```

time: 154 us -> 94.9 us (0.62)
  starting transfers between devices: 52.6 us -> 15.9 us
  waiting for transfers between devices: 28.6 us -> 8.2 us
  matrix products: 17.6 us -> 0 us
  Pallas kernels: 12.1 us -> 21.6 us
  blocking collectives: 34.3 us -> 41.1 us
  other arithmetic: 2.6 us -> 0.08 us
  local copies, waits for them, and re-layouts: 4.76 us -> 6.77 us
    all_to_all x6 -> x0, waiting for transfers between devices: 24.8 us -> none  [exchange(): return lax.all_to_all(a, axis, 0, 0, axis_index_groups=groups, tiled=True)]
    all_to_all x6 -> x0, starting transfers between devices: 21 us -> none  [exchange(): return lax.all_to_all(a, axis, 0, 0, axis_index_groups=groups, tiled=True)]
    dot_general x8 -> x0, matrix products: 17.6 us -> none  [dot(): lax.dot_general(a, b, (dims, ((), ())), precision=precision, preferred_el...]
    ppermute x8, starting transfers between devices: 31.6 us -> 15.9 us  [the longest x6 9.48 us: shift(): return lax.ppermute(a, 'cols', way)]
    pallas_call x2 -> x6, Pallas kernels: 12.1 us -> 21.6 us  [the longest x1 6.24 us: finished(): pl.pallas_call(finish, in_specs=[SCALARS] + [VMEM] * 10 + [pl.BlockSpec(m...]
    all_to_all x3 -> x2, blocking collectives: 34.3 us -> 41.1 us  [exchange(): return lax.all_to_all(a, axis, 0, 0, axis_index_groups=groups, tiled=True)]
    unnamed x16 -> x10, local copies, waits for them, and re-layouts: 0.06 us -> 5.59 us
    ppermute x8, waiting for transfers between devices: 3.79 us -> 8.2 us  [the longest x6 5.5 us: shift(): return lax.ppermute(a, 'cols', way)]
  transfers between devices with their start and end apart: 14 -> 8, of which waited for: 8 -> 5; matrix products, arithmetic and copies ran while one was open for 9% -> 0% of each run, Pallas kernels for 8% -> 4%
where the time goes in v2:
time: 94.9 us; the launch traced here: 94.6 us
  blocking collectives  41.1 us (43%)
  Pallas kernels  21.6 us (23%)
  starting transfers between devices  15.9 us (17%)
  waiting for transfers between devices  8.2 us (9%)
  local copies, waits for them, and re-layouts  6.77 us (7%)
    all_to_all x2, blocking collectives, exchange(): return lax.all_to_all(a, axis, 0, 0, axis_index_groups=groups, tiled=True)  41.1 us
    ppermute x6, starting transfers between devices, shift(): return lax.ppermute(a, 'cols', way)  9.48 us
    ppermute x2, starting transfers between devices, swap(): return lax.ppermute(a, 'rows', CORE_SWAP)  6.43 us
    pallas_call x1, Pallas kernels, finished(): pl.pallas_call(finish, in_specs=[SCALARS] + [VMEM] * 10 + [pl.BlockSpec(m...  6.24 us
    pallas_call x3, Pallas kernels, cross_call(): pl.pallas_call(kernel, grid_spec=pltpu.PrefetchScalarGridSpec(num_scalar_...  5.95 us
    unnamed x10, local copies, waits for them, and re-layouts  5.59 us
    ppermute x6, waiting for transfers between devices, shift(): return lax.ppermute(a, 'cols', way)  5.5 us
    pallas_call x1, Pallas kernels, factor(): pl.pallas_call(second_half, out_shape=(shaped(256, 256), shaped(256, 256)...  5.21 us
  transfers between devices with their start and end apart: 8, of which 5 were waited for; matrix products, arithmetic and copies ran while one was open for 0% of the time, Pallas kernels for 4%

profile of v2, /device:TPU:1, one launch (start us, length us, event | category | flops | bytes accessed | tf_op | source)
XLA Modules:
  0.0 94.6 jit_solution(4950706211099897543)
XLA Ops:
  0.6 1.1 %fusion = (f32[256,256]{1,0:T(8,128)S(1)}, f32[256,256]{1,0:T(8,128)S(1)}) fusion(f32[512,256]{1,0:T(8,128)} %own.1), kind=kLoop, calls=%fused_computation | loop fusion | bytes 1048576 | tf_op jit(solution)/shard_map/slice | solution.py:262
  1.7 3.4 %collective-permute-start.2 = (f32[256,256]{1,0:T(8,128)S(1)}, f32[256,256]{1,0:T(8,128)S(1)}, u32[]{:S(2)}, u32[]{:S(2)}) collective-permute-start(f32[256,256]{1,0:T(8,128)S(1)} %get-tuple-element.29), channel_id=1, source_target_pairs={{0,3},{1,0},{2,1},{3,2},{4,7},{5,4},{6,5},{7,6},{8,11},{9,8},{10,9... | collective-permute-start | bytes 786440 | tf_op jit(solution)/shard_map/ppermute | solution.py:253
  5.1 0.0 collective-permute-start
  5.1 0.2 collective-permute-start.4
  5.3 2.5 %collective-permute-start.5 = (f32[256,256]{1,0:T(8,128)S(1)}, f32[256,256]{1,0:T(8,128)S(1)}, u32[]{:S(2)}, u32[]{:S(2)}) collective-permute-start(f32[256,256]{1,0:T(8,128)S(1)} %get-tuple-element.30), channel_id=1, source_target_pairs={{0,3},{1,0},{2,1},{3,2},{4,7},{5,4},{6,5},{7,6},{8,11},{9,8},{10,9... | collective-permute-start | bytes 786440 | tf_op jit(solution)/shard_map/ppermute | solution.py:253
  7.8 2.3 %collective-permute-done.2.a2 = f32[256,256]{1,0:T(8,128)S(1)} collective-permute-done((f32[256,256]{1,0:T(8,128)S(1)}, f32[256,256]{1,0:T(8,128)S(1)}, u32[]{:S(2)}, u32[]{:S(2)}) %collective-permute-start.2) | collective-permute-done | bytes 262176 | tf_op jit(solution)/shard_map/ppermute | solution.py:253
  10.1 3.4 %collective-permute-start.3 = (f32[256,256]{1,0:T(8,128)S(1)}, f32[256,256]{1,0:T(8,128)S(1)}, u32[]{:S(2)}, u32[]{:S(2)}) collective-permute-start(f32[256,256]{1,0:T(8,128)S(1)} %collective-permute-done.2.a2), channel_id=1, source_target_pairs={{0,3},{1,0},{2,1},{3,2},{4,7},{5,4},{6,5},{7,6},{8,11},{9,8},{10,9... | collective-permute-start | bytes 786440 | tf_op jit(solution)/shard_map/ppermute | solution.py:253
  13.5 0.0 collective-permute-done.b1
  13.5 0.0 collective-permute-start.1
  13.5 0.1 stack.20.places
  13.6 0.0 copy-start
  13.6 2.2 %copy-done = f32[2048,512]{1,0:T(8,128)S(1)} copy-done((f32[2048,512]{1,0:T(8,128)S(1)}, f32[2048,512]{1,0:T(8,128)}, u32[]{:S(2)}) %copy-start) | copy-done | bytes 4194328
  15.8 0.0 copy-start.3
  15.8 1.0 %copy-done.3 = f32[512,256]{1,0:T(8,128)S(1)} copy-done((f32[512,256]{1,0:T(8,128)S(1)}, f32[512,256]{1,0:T(8,128)}, u32[]{:S(2)}) %copy-start.3) | copy-done | bytes 524312
  16.8 0.0 copy-start.1
  16.8 1.6 %cross_own.1 = (f32[256,512]{1,0:T(8,128)S(1)}, f32[256,256]{1,0:T(8,128)S(1)}) custom-call(s32[5]{0:T(128)S(1)} %stack.20.places, f32[512,256]{1,0:T(8,128)S(1)} %copy-done.3, f32[2048,512]{1,0:T(8,128)S(1)} %copy-done), custom_call_target="tpu_custom_call" | custom-call | tf_op jit(solution)/shard_map/cross_own/pallas_call | solution.py:189
  18.5 0.4 collective-permute-done.4.b2
  18.8 0.0 collective-permute-done.5.a1
  18.8 0.2 copy-done.1
  19.0 2.6 %cross_near.1 = (f32[256,512]{1,0:T(8,128)S(1)}, f32[256,256]{1,0:T(8,128)S(1)}) custom-call(s32[5]{0:T(128)S(1)} %stack.20.places, f32[256,256]{1,0:T(8,128)S(1)} %collective-permute-done.b1, f32[256,256]{1,0:T(8,128)S(1)} %collective-permute-done.4.b2, f32[256,256]{1,0:T(8,128)S(1)} %collective-permute-done.5.a1, ...), custom_call_target="tpu_custom_call" | custom-call | tf_op jit(solution)/shard_map/cross_near/pallas_call | solution.py:189
  21.6 0.0 collective-permute-done.3.f2
  21.6 2.8 %collective-permute-done.1.f1 = f32[256,256]{1,0:T(8,128)S(1)} collective-permute-done((f32[256,256]{1,0:T(8,128)S(1)}, f32[256,256]{1,0:T(8,128)S(1)}, u32[]{:S(2)}, u32[]{:S(2)}) %collective-permute-start.1) | collective-permute-done | bytes 262176 | tf_op jit(solution)/shard_map/ppermute | solution.py:253
  24.4 0.0 copy-start.4
  24.4 1.7 %cross_far.1 = (f32[32,24,128]{2,1,0:T(8,128)S(1)}, f32[32,24,128]{2,1,0:T(8,128)S(1)}) custom-call(s32[5]{0:T(128)S(1)} %stack.20.places, f32[256,256]{1,0:T(8,128)S(1)} %collective-permute-done.1.f1, f32[256,256]{1,0:T(8,128)S(1)} %collective-permute-done.3.f2, f32[256,512]{1,0:T(8,128)S(1)} %get-tuple-element.18.cross0, ...), custom_call_target="tpu_custom_call" | custom-call | tf_op jit(solution)/shard_map/cross_far/pallas_call | solution.py:189
  26.2 1.9 %collective-permute-start.6 = (f32[32,24,128]{2,1,0:T(8,128)S(1)}, f32[32,24,128]{2,1,0:T(8,128)S(1)}, u32[]{:S(2)}, u32[]{:S(2)}) collective-permute-start(f32[32,24,128]{2,1,0:T(8,128)S(1)} %get-tuple-element.21), channel_id=1, source_target_pairs={{0,4},{4,0},{8,12},{12,8},{16,20},{20,16},{24,28},{28,24},{32,36},... | collective-permute-start | bytes 1179656 | tf_op jit(solution)/shard_map/ppermute | solution.py:249
  28.1 1.3 %collective-permute-done.6 = f32[32,24,128]{2,1,0:T(8,128)S(1)} collective-permute-done((f32[32,24,128]{2,1,0:T(8,128)S(1)}, f32[32,24,128]{2,1,0:T(8,128)S(1)}, u32[]{:S(2)}, u32[]{:S(2)}) %collective-permute-start.6) | collective-permute-done | bytes 393248 | tf_op jit(solution)/shard_map/ppermute | solution.py:249
  29.5 22.8 %all_to_all.10 = f32[32,24,128]{2,1,0:T(8,128)S(1)} all-to-all(f32[32,24,128]{2,1,0:T(8,128)S(1)} %add.32), channel_id=1, replica_groups={{0,8,16,24,32,40,48,56,64,72,80,88,96,104,112,120,128,136,144,152,160,1..., dimensions={0} | all-to-all | bytes 786432 | tf_op jit(solution)/shard_map/all_to_all | solution.py:28
  52.4 18.3 %all_to_all.11.mine = f32[32,24,128]{2,1,0:T(8,128)S(1)} all-to-all(f32[32,24,128]{2,1,0:T(8,128)S(1)} %broadcast_in_dim.2), channel_id=1, replica_groups={{0,8,16,24,32,40,48,56,64,72,80,88,96,104,112,120,128,136,144,152,160,1..., dimensions={0} | all-to-all | bytes 786432 | tf_op jit(solution)/shard_map/all_to_all | solution.py:28
  70.7 4.5 %collective-permute-start.7 = (f32[32,24,128]{2,1,0:T(8,128)S(1)}, f32[32,24,128]{2,1,0:T(8,128)S(1)}, u32[]{:S(2)}, u32[]{:S(2)}) collective-permute-start(f32[32,24,128]{2,1,0:T(8,128)S(1)} %all_to_all.11.mine), channel_id=1, source_target_pairs={{0,4},{4,0},{8,12},{12,8},{16,20},{20,16},{24,28},{28,24},{32,36},... | collective-permute-start | bytes 1179656 | tf_op jit(solution)/shard_map/ppermute | solution.py:249
  75.2 1.3 %collective-permute-done.7.other = f32[32,24,128]{2,1,0:T(8,128)S(1)} collective-permute-done((f32[32,24,128]{2,1,0:T(8,128)S(1)}, f32[32,24,128]{2,1,0:T(8,128)S(1)}, u32[]{:S(2)}, u32[]{:S(2)}) %collective-permute-start.7) | collective-permute-done | bytes 393248 | tf_op jit(solution)/shard_map/ppermute | solution.py:249
  76.5 4.2 %factor_a.1 = (f32[256,256]{1,0:T(8,128)S(1)}, f32[128,256]{1,0:T(8,128)S(1)}, f32[128,128]{1,0:T(8,128)S(1)}) custom-call(s32[1]{0:T(128)} %bitcast.core, f32[32,24,128]{2,1,0:T(8,128)S(1)} %all_to_all.11.mine, f32[32,24,128]{2,1,0:T(8,128)S(1)} %collective-permute-done.7.other), custom_call_target="tpu_custom_call" | custom-call | tf_op jit(solution)/shard_map/factor_a/pallas_call | solution.py:135
  80.8 5.2 %factor_b.1 = (f32[256,256]{1,0:T(8,128)}, f32[256,256]{1,0:T(8,128)S(1)}) custom-call(f32[256,256]{1,0:T(8,128)S(1)} %get-tuple-element.22.gram, f32[128,256]{1,0:T(8,128)S(1)} %get-tuple-element.23.r0, f32[128,128]{1,0:T(8,128)S(1)} %get-tuple-element.24.x00), custom_call_target="tpu_custom_call" | custom-call | tf_op jit(solution)/shard_map/factor_b/pallas_call | solution.py:142
  86.0 0.0 copy-done.4
  86.0 0.0 copy-start.2
  86.0 2.2 %copy-done.2 = f32[2048,512]{1,0:T(8,128)S(1)} copy-done((f32[2048,512]{1,0:T(8,128)S(1)}, f32[2048,512]{1,0:T(8,128)}, u32[]{:S(2)}) %copy-start.2) | copy-done | bytes 4194328
  88.2 6.2 %finish.1 = (f32[256,512]{1,0:T(8,128)}, f32[2048,512]{1,0:T(8,128)}) custom-call(s32[5]{0:T(128)S(1)} %stack.20.places, f32[256,256]{1,0:T(8,128)S(1)} %get-tuple-element.26.inverse, f32[32,24,128]{2,1,0:T(8,128)S(1)} %all_to_all.11.mine, f32[32,24,128]{2,1,0:T(8,128)S(1)} %collective-permute-done.7.other, f32[512,256]{1,0:T(8,128)S(1)} %copy-done.4, ...), custom_call_target="tpu_custom_call" | custom-call | tf_op jit(solution)/shard_map/finish/pallas_call | solution.py:235
  (3 shorter events, 0.1 us)
Async XLA Ops:
  1.7 8.4 %collective-permute-start.2 = (f32[256,256]{1,0:T(8,128)S(1)}, f32[256,256]{1,0:T(8,128)S(1)}, u32[]{:S(2)}, u32[]{:S(2)}) collective-permute-start(f32[256,256]{1,0:T(8,128)S(1)} %get-tuple-element.29), channel_id=1, source_target_pairs={{0,3},{1,0},{2,1},{3,2},{4,7},{5,4},{6,5},{7,6},{8,11},{9,8},{10,9... | collective-permute-start | bytes 786440 | tf_op jit(solution)/shard_map/ppermute | solution.py:253
  5.1 8.4 %collective-permute-start = (f32[256,256]{1,0:T(8,128)S(1)}, f32[256,256]{1,0:T(8,128)S(1)}, u32[]{:S(2)}, u32[]{:S(2)}) collective-permute-start(f32[256,256]{1,0:T(8,128)S(1)} %get-tuple-element.30), channel_id=1, source_target_pairs={{0,1},{1,2},{2,3},{3,0},{4,5},{5,6},{6,7},{7,4},{8,9},{9,10},{10,1... | collective-permute-start | bytes 786440 | tf_op jit(solution)/shard_map/ppermute | solution.py:253
  5.1 13.7 %collective-permute-start.4 = (f32[256,256]{1,0:T(8,128)S(1)}, f32[256,256]{1,0:T(8,128)S(1)}, u32[]{:S(2)}, u32[]{:S(2)}) collective-permute-start(f32[256,256]{1,0:T(8,128)S(1)} %get-tuple-element.29), channel_id=1, source_target_pairs={{0,1},{1,2},{2,3},{3,0},{4,5},{5,6},{6,7},{7,4},{8,9},{9,10},{10,1... | collective-permute-start | bytes 786440 | tf_op jit(solution)/shard_map/ppermute | solution.py:253
  5.3 13.5 %collective-permute-start.5 = (f32[256,256]{1,0:T(8,128)S(1)}, f32[256,256]{1,0:T(8,128)S(1)}, u32[]{:S(2)}, u32[]{:S(2)}) collective-permute-start(f32[256,256]{1,0:T(8,128)S(1)} %get-tuple-element.30), channel_id=1, source_target_pairs={{0,3},{1,0},{2,1},{3,2},{4,7},{5,4},{6,5},{7,6},{8,11},{9,8},{10,9... | collective-permute-start | bytes 786440 | tf_op jit(solution)/shard_map/ppermute | solution.py:253
  10.1 11.5 %collective-permute-start.3 = (f32[256,256]{1,0:T(8,128)S(1)}, f32[256,256]{1,0:T(8,128)S(1)}, u32[]{:S(2)}, u32[]{:S(2)}) collective-permute-start(f32[256,256]{1,0:T(8,128)S(1)} %collective-permute-done.2.a2), channel_id=1, source_target_pairs={{0,3},{1,0},{2,1},{3,2},{4,7},{5,4},{6,5},{7,6},{8,11},{9,8},{10,9... | collective-permute-start | bytes 786440 | tf_op jit(solution)/shard_map/ppermute | solution.py:253
  13.5 11.0 %collective-permute-start.1 = (f32[256,256]{1,0:T(8,128)S(1)}, f32[256,256]{1,0:T(8,128)S(1)}, u32[]{:S(2)}, u32[]{:S(2)}) collective-permute-start(f32[256,256]{1,0:T(8,128)S(1)} %collective-permute-done.b1), channel_id=1, source_target_pairs={{0,1},{1,2},{2,3},{3,0},{4,5},{5,6},{6,7},{7,4},{8,9},{9,10},{10,1... | collective-permute-start | bytes 786440 | tf_op jit(solution)/shard_map/ppermute | solution.py:253
  13.6 2.2 %copy-start = (f32[2048,512]{1,0:T(8,128)S(1)}, f32[2048,512]{1,0:T(8,128)}, u32[]{:S(2)}) copy-start(f32[2048,512]{1,0:T(8,128)} %trailing.1) | copy-start | bytes 12582916
  15.8 1.0 %copy-start.3 = (f32[512,256]{1,0:T(8,128)S(1)}, f32[512,256]{1,0:T(8,128)}, u32[]{:S(2)}) copy-start(f32[512,256]{1,0:T(8,128)} %own.1) | copy-start | bytes 1572868
  16.8 2.2 %copy-start.1 = (f32[2048,512]{1,0:T(8,128)S(1)}, f32[2048,512]{1,0:T(8,128)}, u32[]{:S(2)}) copy-start(f32[2048,512]{1,0:T(8,128)} %trailing.1) | copy-start | bytes 12582916
  24.4 61.6 %copy-start.4 = (f32[512,256]{1,0:T(8,128)S(1)}, f32[512,256]{1,0:T(8,128)}, u32[]{:S(2)}) copy-start(f32[512,256]{1,0:T(8,128)} %own.1) | copy-start | bytes 1572868
  26.2 3.2 %collective-permute-start.6 = (f32[32,24,128]{2,1,0:T(8,128)S(1)}, f32[32,24,128]{2,1,0:T(8,128)S(1)}, u32[]{:S(2)}, u32[]{:S(2)}) collective-permute-start(f32[32,24,128]{2,1,0:T(8,128)S(1)} %get-tuple-element.21), channel_id=1, source_target_pairs={{0,4},{4,0},{8,12},{12,8},{16,20},{20,16},{24,28},{28,24},{32,36},... | collective-permute-start | bytes 1179656 | tf_op jit(solution)/shard_map/ppermute | solution.py:249
  70.7 5.9 %collective-permute-start.7 = (f32[32,24,128]{2,1,0:T(8,128)S(1)}, f32[32,24,128]{2,1,0:T(8,128)S(1)}, u32[]{:S(2)}, u32[]{:S(2)}) collective-permute-start(f32[32,24,128]{2,1,0:T(8,128)S(1)} %all_to_all.11.mine), channel_id=1, source_target_pairs={{0,4},{4,0},{8,12},{12,8},{16,20},{20,16},{24,28},{28,24},{32,36},... | collective-permute-start | bytes 1179656 | tf_op jit(solution)/shard_map/ppermute | solution.py:249
  86.0 2.2 %copy-start.2 = (f32[2048,512]{1,0:T(8,128)S(1)}, f32[2048,512]{1,0:T(8,128)}, u32[]{:S(2)}) copy-start(f32[2048,512]{1,0:T(8,128)} %trailing.1) | copy-start | bytes 12582916

commit v3 on v2

v3 whole, which is shorter than its diff:
```python
import jax
import jax.numpy as jnp
from jax import lax
from jax.experimental import pallas as pl
from jax.experimental.pallas import tpu as pltpu
from jax.sharding import PartitionSpec as P

NY, NZ, NC, NX = 4, 8, 2, 4
HIGHEST = lax.Precision.HIGHEST
F32 = jnp.float32


def row_id(y, z, c):
    return (y * NZ + z) * NC + c


GROUP_YZ = [[row_id(y, z, c) for y in range(NY) for z in range(NZ)] for c in range(NC)]
CORE_SWAP = [(i, i ^ 1) for i in range(NY * NZ * NC)]
X_UP = [(i, (i + 1) % NX) for i in range(NX)]
X_DOWN = [(i, (i - 1) % NX) for i in range(NX)]


def dot(a, b, dims=((1,), (0,)), precision=HIGHEST):
    return lax.dot_general(a, b, (dims, ((), ())), precision=precision, preferred_element_type=F32)


def exchange(a, axis, groups=None):
    return lax.all_to_all(a, axis, 0, 0, axis_index_groups=groups, tiled=True)


def split(a):
    hi = a.astype(jnp.bfloat16)
    return hi, (a - hi.astype(F32)).astype(jnp.bfloat16)


def product(a, b):
    (ah, al), (bh, bl) = a, b
    return dot(ah, bh, precision=None) + (dot(ah, bl, precision=None) + dot(al, bh, precision=None))


def copies(a, n):
    return jnp.broadcast_to(a[None], (n, *a.shape))


def spread(slab, row):
    return jnp.broadcast_to(slab[row : row + 1, :], slab.shape)


def factor_block(d):
    n = 128
    slabs = n // 8
    D = [d[8 * s : 8 * s + 8, :] for s in range(slabs)]
    sub = lax.broadcasted_iota(jnp.int32, (8, n), 0)
    lane = lax.broadcasted_iota(jnp.int32, (8, n), 1)
    E = [(lane == sub + 8 * s).astype(F32) for s in range(slabs)]
    R = []
    for g in range(slabs):
        C = [[jnp.broadcast_to(D[s][:, 8 * g + k : 8 * g + k + 1], (8, n)) for s in range(g, slabs)] for k in range(8)]
        scale = jnp.zeros((8, n), F32)
        M = []
        piv = spread(C[0][0], 0)
        for j in range(8):
            inv = 1.0 / piv
            if j < 7:
                after = spread(C[j + 1][0], j + 1) - (spread(C[j][0], j + 1) * inv) * spread(C[j + 1][0], j)
            root = lax.rsqrt(piv)
            root = root * (1.5 - 0.5 * piv * root * root)
            scale = jnp.where(sub == j, root, scale)
            M.append([C[j][t] * inv if t else jnp.where(sub > j, C[j][t] * inv, 0.0) for t in range(slabs - g)])
            for k in range(j + 1, 8):
                top = spread(C[k][0], j)
                for t in range(slabs - g):
                    C[k][t] = C[k][t] - M[j][t] * top
            piv = after
        for j in range(8):
            dj = spread(D[g], j)
            ej = spread(E[g], j)
            for t in range(slabs - g):
                D[g + t] = D[g + t] - M[j][t] * dj
                E[g + t] = E[g + t] - M[j][t] * ej
        R.append(jnp.where(lane >= sub + 8 * g, D[g] * scale, 0.0))
        E[g] = E[g] * scale
    return jnp.concatenate(R, axis=0), jnp.concatenate(E, axis=0)


def cut(src, start, out, first):
    across = src.shape[1] // 128
    h = 4 * across
    for p in range(32):
        r, c = divmod(p, across)
        out[p, first : first + h, :] = src[pl.ds(start + r * h, h), 128 * c : 128 * c + 128]


def paste(pieces, start, dst, first):
    across = dst.shape[1] // 128
    h = 4 * across
    for p in range(32):
        r, c = divmod(p, across)
        dst[pl.ds(start + r * h, h), 128 * c : 128 * c + 128] = pieces[p, first : first + h, :]


def starts(core):
    mine = pl.multiple_of(core[0] * 128, 128)
    return mine, pl.multiple_of(128 - mine, 128)


SMALL = pltpu.CompilerParams(vmem_limit_bytes=24 * 2**20)
FLOPS = 4 * 10**9
SCALARS = pl.BlockSpec(memory_space=pltpu.SMEM)
VMEM = pl.BlockSpec(memory_space=pltpu.VMEM)


def shaped(*shape):
    return jax.ShapeDtypeStruct(shape, F32)


def factor_kernel(core, mine, other, r, x, gram):
    m, o = starts([core[0]])
    paste(mine, m, gram, 16)
    paste(other, o, gram, 16)
    r00, x00 = factor_block(gram[:128, :128])
    r01 = dot(x00, gram[:128, 128:])
    r01t = r01.T
    r11, x11 = factor_block(gram[128:, 128:] - dot(r01t, r01))
    zero = jnp.zeros((128, 128), F32)
    r[:128, :128] = r00
    r[:128, 128:] = r01
    r[128:, :128] = zero
    r[128:, 128:] = r11
    x[:128, :128] = x00
    x[:128, 128:] = zero
    x[128:, :128] = -dot(x11, dot(r01t, x00))
    x[128:, 128:] = x11


def factor(core, mine, other):
    return pl.pallas_call(
        factor_kernel,
        out_shape=(shaped(256, 256), shaped(256, 256)),
        in_specs=[SCALARS, VMEM, VMEM],
        scratch_shapes=[pltpu.VMEM((256, 256), F32)],
        compiler_params=SMALL,
        cost_estimate=pl.CostEstimate(flops=FLOPS, bytes_accessed=2**20, transcendentals=0),
        name="factor",
    )(core, mine, other)


def accumulate(pieces, trails):
    cross, gram = 0.0, 0.0
    for piece, trail in zip(pieces, trails):
        flipped, straight = split(piece.T), split(piece)
        cross = cross + product(flipped, split(trail))
        gram = gram + (product(flipped, straight) + dot(flipped[1], straight[1], precision=None))
    return cross, gram


def rows_at(ref, place, first=0, n=512):
    return ref[pl.ds(pl.multiple_of(place * 512 + first, 256), n), :]


def cross_own(places, panel, trailing, keep, cross, gram):
    keep[...] = trailing[...]
    cross[...], gram[...] = accumulate([panel[...]], [rows_at(trailing, places[0])])


def cross_near(places, b1, b2, a1, a2, keep, cross0, gram0, cross, gram):
    trails = [rows_at(keep, places[k], first, 256) for k in (1, 2) for first in (0, 256)]
    c, g = accumulate([b1[...], b2[...], a1[...], a2[...]], trails)
    cross[...] = cross0[...] + c
    gram[...] = gram0[...] + g


def cross_far(places, f1, f2, keep, cross0, gram0, mine, other, cross, gram):
    trails = [rows_at(keep, places[3], first, 256) for first in (0, 256)]
    c, g = accumulate([f1[...], f2[...]], trails)
    cross[...] = cross0[...] + c
    gram[...] = gram0[...] + g
    m, o = starts([places[4]])
    cut(cross, m, mine, 0)
    cut(gram, m, mine, 16)
    cut(cross, o, other, 0)
    cut(gram, o, other, 16)


def call(kernel, places, arrays, outs, flops, scratch=()):
    return pl.pallas_call(
        kernel,
        in_specs=[SCALARS] + [VMEM] * len(arrays),
        out_specs=[VMEM] * len(outs),
        out_shape=outs,
        scratch_shapes=scratch,
        compiler_params=SMALL,
        cost_estimate=pl.CostEstimate(flops=flops, bytes_accessed=2**21, transcendentals=0),
        name=kernel.__name__,
    )(places, *arrays)


def finish(places, inverse, mine, other, own, b1, b2, a1, a2, f1, f2, trailing, projected, updated, cross, result, writes):
    m, o = starts([places[4]])
    paste(mine, m, cross, 0)
    paste(other, o, cross, 0)
    p = dot(inverse[...], cross[...])
    projected[...] = p
    w = split(dot(inverse[...], p, ((0,), (0,))))
    moves = []
    for k, parts in enumerate([(own,), (b1, b2), (a1, a2), (f1, f2)]):
        n = 512 // len(parts)
        for i, part in enumerate(parts):
            result[k, n * i : n * i + n, :] = rows_at(trailing, places[k], n * i, n) - product(split(part[...]), w)
        rows = pl.ds(pl.multiple_of(places[k] * 512, 512), 512)
        moves.append(pltpu.make_async_copy(result.at[k], updated.at[rows, :], writes.at[k]))
        moves[k].start()
    for move in moves:
        move.wait()


def finished(places, arrays):
    return pl.pallas_call(
        finish,
        in_specs=[SCALARS] + [VMEM] * len(arrays),
        out_specs=[VMEM, pl.BlockSpec(memory_space=pltpu.HBM)],
        out_shape=[shaped(256, 512), shaped(2048, 512)],
        scratch_shapes=[pltpu.VMEM((256, 512), F32), pltpu.VMEM((4, 512, 512), F32), pltpu.SemaphoreType.DMA((4,))],
        compiler_params=SMALL,
        name="finish",
    )(places, *arrays)


def swap(a):
    return lax.ppermute(a, "rows", CORE_SWAP)


def shift(a, way):
    return lax.ppermute(a, "cols", way)


def shards(panel, trailing):
    x = lax.axis_index("cols")
    core = lax.axis_index("rows") % 2
    core_word = core.reshape(1)
    places = jnp.stack([x, (x + 3) % 4, (x + 1) % 4, (x + 2) % 4, core])

    top, low = panel[:256], panel[256:]
    b1 = shift(top, X_UP)
    a2 = shift(low, X_DOWN)
    b2 = shift(low, X_UP)
    a1 = shift(top, X_DOWN)
    sums = [shaped(256, 512), shaped(256, 256)]
    keep, *part = call(cross_own, places, [panel, trailing], [shaped(2048, 512), *sums], 10**9)
    b1, a2, keep, *part = lax.optimization_barrier((b1, a2, keep, *part))
    f1 = shift(b1, X_UP)
    f2 = shift(a2, X_DOWN)
    part = call(cross_near, places, [b1, b2, a1, a2, keep, *part], sums, 10**8)
    halves = [shaped(32, 24, 128)] * 2
    scratch = [pltpu.VMEM((256, 512), F32), pltpu.VMEM((256, 256), F32)]
    mine, other = call(cross_far, places, [f1, f2, keep, *part], halves, 10**8, scratch)
    total = exchange(mine + swap(other), "rows", GROUP_YZ).sum(0)
    mine = exchange(copies(total, 32), "rows", GROUP_YZ)
    other = swap(mine)
    rfactor, inverse = factor(core_word, mine, other)
    projected, updated = finished(places, [inverse, mine, other, panel, b1, b2, a1, a2, f1, f2, trailing])
    return rfactor, projected, updated


def solution(mesh):
    placed = (P(("rows", "cols"), None), P("rows", "cols"))
    return jax.shard_map(
        shards,
        mesh=mesh,
        in_specs=placed,
        out_specs=(P(), P(None, "cols"), P("rows", "cols")),
        check_vma=False,
    )
```

time: 94.9 us -> 91 us (0.959)
  local copies, waits for them, and re-layouts: 6.77 us -> 4.42 us
  Pallas kernels: 21.6 us -> 19.6 us
  waiting for transfers between devices: 8.2 us -> 9.44 us
    unnamed x10 -> x8, local copies, waits for them, and re-layouts: 5.59 us -> 3.24 us
    pallas_call x6 -> x5, Pallas kernels: 21.6 us -> 19.6 us  [the longest x1 8.8 us: factor(): pl.pallas_call(factor_kernel, out_shape=(shaped(256, 256), shaped(256, 25...]
    ppermute x6, waiting for transfers between devices: 5.5 us -> 6.74 us  [shift(): return lax.ppermute(a, 'cols', way)]
where the time goes in v3:
time: 91 us; the launch traced here: 90.7 us
  blocking collectives  41.1 us (45%)
  Pallas kernels  19.6 us (22%)
  starting transfers between devices  15.2 us (17%)
  waiting for transfers between devices  9.44 us (10%)
  local copies, waits for them, and re-layouts  4.42 us (5%)
    all_to_all x2, blocking collectives, exchange(): return lax.all_to_all(a, axis, 0, 0, axis_index_groups=groups, tiled=True)  41.1 us
    pallas_call x1, Pallas kernels, factor(): pl.pallas_call(factor_kernel, out_shape=(shaped(256, 256), shaped(256, 25...  8.8 us
    ppermute x6, starting transfers between devices, shift(): return lax.ppermute(a, 'cols', way)  8.75 us
    ppermute x6, waiting for transfers between devices, shift(): return lax.ppermute(a, 'cols', way)  6.74 us
    ppermute x2, starting transfers between devices, swap(): return lax.ppermute(a, 'rows', CORE_SWAP)  6.43 us
    pallas_call x3, Pallas kernels, call(): pl.pallas_call(kernel, in_specs=[SCALARS] + [VMEM] * len(arrays), out_spe...  5.45 us
    pallas_call x1, Pallas kernels, finished(): pl.pallas_call(finish, in_specs=[SCALARS] + [VMEM] * len(arrays), out_spe...  5.39 us
    unnamed x8, local copies, waits for them, and re-layouts  3.24 us
  transfers between devices with their start and end apart: 8, of which 5 were waited for; matrix products, arithmetic and copies ran while one was open for 0% of the time, Pallas kernels for 4%

profile of v3, /device:TPU:1, one launch (start us, length us, event | category | flops | bytes accessed | tf_op | source)
XLA Modules:
  0.0 90.7 jit_solution(16545287316312111470)
XLA Ops:
  0.6 1.1 %fusion = (f32[256,256]{1,0:T(8,128)S(1)}, f32[256,256]{1,0:T(8,128)S(1)}) fusion(f32[512,256]{1,0:T(8,128)} %own.1), kind=kLoop, calls=%fused_computation | loop fusion | bytes 1048576 | tf_op jit(solution)/shard_map/slice | solution.py:243
  1.7 3.4 %collective-permute-start.1 = (f32[256,256]{1,0:T(8,128)S(1)}, f32[256,256]{1,0:T(8,128)S(1)}, u32[]{:S(2)}, u32[]{:S(2)}) collective-permute-start(f32[256,256]{1,0:T(8,128)S(1)} %get-tuple-element.35), channel_id=1, source_target_pairs={{0,3},{1,0},{2,1},{3,2},{4,7},{5,4},{6,5},{7,6},{8,11},{9,8},{10,9... | collective-permute-start | bytes 786440 | tf_op jit(solution)/shard_map/ppermute | solution.py:234
  5.1 0.0 collective-permute-start
  5.1 0.2 collective-permute-start.4
  5.3 2.5 %collective-permute-start.5 = (f32[256,256]{1,0:T(8,128)S(1)}, f32[256,256]{1,0:T(8,128)S(1)}, u32[]{:S(2)}, u32[]{:S(2)}) collective-permute-start(f32[256,256]{1,0:T(8,128)S(1)} %get-tuple-element.36), channel_id=1, source_target_pairs={{0,3},{1,0},{2,1},{3,2},{4,7},{5,4},{6,5},{7,6},{8,11},{9,8},{10,9... | collective-permute-start | bytes 786440 | tf_op jit(solution)/shard_map/ppermute | solution.py:234
  7.8 0.1 stack.20.places
  7.9 0.0 copy-start
  7.9 2.2 %copy-done = f32[2048,512]{1,0:T(8,128)S(1)} copy-done((f32[2048,512]{1,0:T(8,128)S(1)}, f32[2048,512]{1,0:T(8,128)}, u32[]{:S(2)}) %copy-start) | copy-done | bytes 4194328
  10.0 0.0 copy-start.2
  10.0 1.0 %copy-done.2 = f32[512,256]{1,0:T(8,128)S(1)} copy-done((f32[512,256]{1,0:T(8,128)S(1)}, f32[512,256]{1,0:T(8,128)}, u32[]{:S(2)}) %copy-start.2) | copy-done | bytes 524312
  11.1 1.7 %cross_own.1 = (f32[2048,512]{1,0:T(8,128)S(1)}, f32[256,512]{1,0:T(8,128)S(1)}, f32[256,256]{1,0:T(8,128)S(1)}) custom-call(s32[5]{0:T(128)S(1)} %stack.20.places, f32[512,256]{1,0:T(8,128)S(1)} %copy-done.2, f32[2048,512]{1,0:T(8,128)S(1)} %copy-done), custom_call_target="tpu_custom_call" | custom-call | flops 1000000000 | bytes 2097152 | tf_op jit(solution)/shard_map/cross_own/pallas_call | solution.py:186
  12.8 0.0 collective-permute-done.1.a2
  12.8 0.4 collective-permute-done.b1
  13.2 0.0 collective-permute-start.2
  13.2 2.7 %collective-permute-start.3 = (f32[256,256]{1,0:T(8,128)S(1)}, f32[256,256]{1,0:T(8,128)S(1)}, u32[]{:S(2)}, u32[]{:S(2)}) collective-permute-start(f32[256,256]{1,0:T(8,128)S(1)} %collective-permute-done.1.a2), channel_id=1, source_target_pairs={{0,3},{1,0},{2,1},{3,2},{4,7},{5,4},{6,5},{7,6},{8,11},{9,8},{10,9... | collective-permute-start | bytes 786440 | tf_op jit(solution)/shard_map/ppermute | solution.py:234
  15.9 2.9 %collective-permute-done.4.b2 = f32[256,256]{1,0:T(8,128)S(1)} collective-permute-done((f32[256,256]{1,0:T(8,128)S(1)}, f32[256,256]{1,0:T(8,128)S(1)}, u32[]{:S(2)}, u32[]{:S(2)}) %collective-permute-start.4) | collective-permute-done | bytes 262176 | tf_op jit(solution)/shard_map/ppermute | solution.py:234
  18.8 0.0 collective-permute-done.5.a1
  18.8 2.2 %cross_near.1 = (f32[256,512]{1,0:T(8,128)S(1)}, f32[256,256]{1,0:T(8,128)S(1)}) custom-call(s32[5]{0:T(128)S(1)} %stack.20.places, f32[256,256]{1,0:T(8,128)S(1)} %collective-permute-done.b1, f32[256,256]{1,0:T(8,128)S(1)} %collective-permute-done.4.b2, f32[256,256]{1,0:T(8,128)S(1)} %collective-permute-done.5.a1, ...), custom_call_target="tpu_custom_call" | custom-call | flops 100000000 | bytes 2097152 | tf_op jit(solution)/shard_map/cross_near/pallas_call | solution.py:186
  21.0 3.4 %collective-permute-done.2.f1 = f32[256,256]{1,0:T(8,128)S(1)} collective-permute-done((f32[256,256]{1,0:T(8,128)S(1)}, f32[256,256]{1,0:T(8,128)S(1)}, u32[]{:S(2)}, u32[]{:S(2)}) %collective-permute-start.2) | collective-permute-done | bytes 262176 | tf_op jit(solution)/shard_map/ppermute | solution.py:234
  24.4 0.0 collective-permute-done.3.f2
  24.4 1.5 %cross_far.1 = (f32[32,24,128]{2,1,0:T(8,128)S(1)}, f32[32,24,128]{2,1,0:T(8,128)S(1)}) custom-call(s32[5]{0:T(128)S(1)} %stack.20.places, f32[256,256]{1,0:T(8,128)S(1)} %collective-permute-done.2.f1, f32[256,256]{1,0:T(8,128)S(1)} %collective-permute-done.3.f2, f32[2048,512]{1,0:T(8,128)S(1)} %get-tuple-element.24.keep, ...), custom_call_target="tpu_custom_call" | custom-call | flops 100000000 | bytes 2097152 | tf_op jit(solution)/shard_map/cross_far/pallas_call | solution.py:186
  26.0 1.9 %collective-permute-start.6 = (f32[32,24,128]{2,1,0:T(8,128)S(1)}, f32[32,24,128]{2,1,0:T(8,128)S(1)}, u32[]{:S(2)}, u32[]{:S(2)}) collective-permute-start(f32[32,24,128]{2,1,0:T(8,128)S(1)} %get-tuple-element.30), channel_id=1, source_target_pairs={{0,4},{4,0},{8,12},{12,8},{16,20},{20,16},{24,28},{28,24},{32,36},... | collective-permute-start | bytes 1179656 | tf_op jit(solution)/shard_map/ppermute | solution.py:230
  27.9 1.3 %collective-permute-done.6 = f32[32,24,128]{2,1,0:T(8,128)S(1)} collective-permute-done((f32[32,24,128]{2,1,0:T(8,128)S(1)}, f32[32,24,128]{2,1,0:T(8,128)S(1)}, u32[]{:S(2)}, u32[]{:S(2)}) %collective-permute-start.6) | collective-permute-done | bytes 393248 | tf_op jit(solution)/shard_map/ppermute | solution.py:230
  29.3 22.8 %all_to_all.10 = f32[32,24,128]{2,1,0:T(8,128)S(1)} all-to-all(f32[32,24,128]{2,1,0:T(8,128)S(1)} %add.32), channel_id=1, replica_groups={{0,8,16,24,32,40,48,56,64,72,80,88,96,104,112,120,128,136,144,152,160,1..., dimensions={0} | all-to-all | bytes 786432 | tf_op jit(solution)/shard_map/all_to_all | solution.py:28
  52.2 18.3 %all_to_all.11.mine = f32[32,24,128]{2,1,0:T(8,128)S(1)} all-to-all(f32[32,24,128]{2,1,0:T(8,128)S(1)} %broadcast_in_dim.2), channel_id=1, replica_groups={{0,8,16,24,32,40,48,56,64,72,80,88,96,104,112,120,128,136,144,152,160,1..., dimensions={0} | all-to-all | bytes 786432 | tf_op jit(solution)/shard_map/all_to_all | solution.py:28
  70.5 0.0 copy-start.1
  70.5 0.0 copy-start.3
  70.5 4.5 %collective-permute-start.7 = (f32[32,24,128]{2,1,0:T(8,128)S(1)}, f32[32,24,128]{2,1,0:T(8,128)S(1)}, u32[]{:S(2)}, u32[]{:S(2)}) collective-permute-start(f32[32,24,128]{2,1,0:T(8,128)S(1)} %all_to_all.11.mine), channel_id=1, source_target_pairs={{0,4},{4,0},{8,12},{12,8},{16,20},{20,16},{24,28},{28,24},{32,36},... | collective-permute-start | bytes 1179656 | tf_op jit(solution)/shard_map/ppermute | solution.py:230
  75.0 1.3 %collective-permute-done.7.other = f32[32,24,128]{2,1,0:T(8,128)S(1)} collective-permute-done((f32[32,24,128]{2,1,0:T(8,128)S(1)}, f32[32,24,128]{2,1,0:T(8,128)S(1)}, u32[]{:S(2)}, u32[]{:S(2)}) %collective-permute-start.7) | collective-permute-done | bytes 393248 | tf_op jit(solution)/shard_map/ppermute | solution.py:230
  76.4 8.8 %factor.1 = (f32[256,256]{1,0:T(8,128)}, f32[256,256]{1,0:T(8,128)S(1)}) custom-call(s32[1]{0:T(128)} %bitcast.core, f32[32,24,128]{2,1,0:T(8,128)S(1)} %all_to_all.11.mine, f32[32,24,128]{2,1,0:T(8,128)S(1)} %collective-permute-done.7.other), custom_call_target="tpu_custom_call" | custom-call | flops 4000000000 | bytes 1048576 | tf_op jit(solution)/shard_map/factor/pallas_call | solution.py:137
  85.2 0.0 copy-done.1
  85.2 0.0 copy-done.3
  85.2 5.4 %finish.1 = (f32[256,512]{1,0:T(8,128)}, f32[2048,512]{1,0:T(8,128)}) custom-call(s32[5]{0:T(128)S(1)} %stack.20.places, f32[256,256]{1,0:T(8,128)S(1)} %get-tuple-element.32.inverse, f32[32,24,128]{2,1,0:T(8,128)S(1)} %all_to_all.11.mine, f32[32,24,128]{2,1,0:T(8,128)S(1)} %collective-permute-done.7.other, f32[512,256]{1,0:T(8,128)S(1)} %copy-done.3, ...), custom_call_target="tpu_custom_call" | custom-call | tf_op jit(solution)/shard_map/finish/pallas_call | solution.py:218
  (3 shorter events, 0.1 us)
Async XLA Ops:
  1.7 11.1 %collective-permute-start.1 = (f32[256,256]{1,0:T(8,128)S(1)}, f32[256,256]{1,0:T(8,128)S(1)}, u32[]{:S(2)}, u32[]{:S(2)}) collective-permute-start(f32[256,256]{1,0:T(8,128)S(1)} %get-tuple-element.35), channel_id=1, source_target_pairs={{0,3},{1,0},{2,1},{3,2},{4,7},{5,4},{6,5},{7,6},{8,11},{9,8},{10,9... | collective-permute-start | bytes 786440 | tf_op jit(solution)/shard_map/ppermute | solution.py:234
  5.1 8.1 %collective-permute-start = (f32[256,256]{1,0:T(8,128)S(1)}, f32[256,256]{1,0:T(8,128)S(1)}, u32[]{:S(2)}, u32[]{:S(2)}) collective-permute-start(f32[256,256]{1,0:T(8,128)S(1)} %get-tuple-element.36), channel_id=1, source_target_pairs={{0,1},{1,2},{2,3},{3,0},{4,5},{5,6},{6,7},{7,4},{8,9},{9,10},{10,1... | collective-permute-start | bytes 786440 | tf_op jit(solution)/shard_map/ppermute | solution.py:234
  5.1 13.7 %collective-permute-start.4 = (f32[256,256]{1,0:T(8,128)S(1)}, f32[256,256]{1,0:T(8,128)S(1)}, u32[]{:S(2)}, u32[]{:S(2)}) collective-permute-start(f32[256,256]{1,0:T(8,128)S(1)} %get-tuple-element.35), channel_id=1, source_target_pairs={{0,1},{1,2},{2,3},{3,0},{4,5},{5,6},{6,7},{7,4},{8,9},{9,10},{10,1... | collective-permute-start | bytes 786440 | tf_op jit(solution)/shard_map/ppermute | solution.py:234
  5.3 13.5 %collective-permute-start.5 = (f32[256,256]{1,0:T(8,128)S(1)}, f32[256,256]{1,0:T(8,128)S(1)}, u32[]{:S(2)}, u32[]{:S(2)}) collective-permute-start(f32[256,256]{1,0:T(8,128)S(1)} %get-tuple-element.36), channel_id=1, source_target_pairs={{0,3},{1,0},{2,1},{3,2},{4,7},{5,4},{6,5},{7,6},{8,11},{9,8},{10,9... | collective-permute-start | bytes 786440 | tf_op jit(solution)/shard_map/ppermute | solution.py:234
  7.9 2.2 %copy-start = (f32[2048,512]{1,0:T(8,128)S(1)}, f32[2048,512]{1,0:T(8,128)}, u32[]{:S(2)}) copy-start(f32[2048,512]{1,0:T(8,128)} %trailing.3) | copy-start | bytes 12582916
  10.0 1.0 %copy-start.2 = (f32[512,256]{1,0:T(8,128)S(1)}, f32[512,256]{1,0:T(8,128)}, u32[]{:S(2)}) copy-start(f32[512,256]{1,0:T(8,128)} %own.1) | copy-start | bytes 1572868
  13.2 11.2 %collective-permute-start.2 = (f32[256,256]{1,0:T(8,128)S(1)}, f32[256,256]{1,0:T(8,128)S(1)}, u32[]{:S(2)}, u32[]{:S(2)}) collective-permute-start(f32[256,256]{1,0:T(8,128)S(1)} %collective-permute-done.b1), channel_id=1, source_target_pairs={{0,1},{1,2},{2,3},{3,0},{4,5},{5,6},{6,7},{7,4},{8,9},{9,10},{10,1... | collective-permute-start | bytes 786440 | tf_op jit(solution)/shard_map/ppermute | solution.py:234
  13.2 11.2 %collective-permute-start.3 = (f32[256,256]{1,0:T(8,128)S(1)}, f32[256,256]{1,0:T(8,128)S(1)}, u32[]{:S(2)}, u32[]{:S(2)}) collective-permute-start(f32[256,256]{1,0:T(8,128)S(1)} %collective-permute-done.1.a2), channel_id=1, source_target_pairs={{0,3},{1,0},{2,1},{3,2},{4,7},{5,4},{6,5},{7,6},{8,11},{9,8},{10,9... | collective-permute-start | bytes 786440 | tf_op jit(solution)/shard_map/ppermute | solution.py:234
  26.0 3.2 %collective-permute-start.6 = (f32[32,24,128]{2,1,0:T(8,128)S(1)}, f32[32,24,128]{2,1,0:T(8,128)S(1)}, u32[]{:S(2)}, u32[]{:S(2)}) collective-permute-start(f32[32,24,128]{2,1,0:T(8,128)S(1)} %get-tuple-element.30), channel_id=1, source_target_pairs={{0,4},{4,0},{8,12},{12,8},{16,20},{20,16},{24,28},{28,24},{32,36},... | collective-permute-start | bytes 1179656 | tf_op jit(solution)/shard_map/ppermute | solution.py:230
  70.5 14.7 %copy-start.1 = (f32[2048,512]{1,0:T(8,128)S(1)}, f32[2048,512]{1,0:T(8,128)}, u32[]{:S(2)}) copy-start(f32[2048,512]{1,0:T(8,128)} %trailing.3) | copy-start | bytes 12582916
  70.5 14.7 %copy-start.3 = (f32[512,256]{1,0:T(8,128)S(1)}, f32[512,256]{1,0:T(8,128)}, u32[]{:S(2)}) copy-start(f32[512,256]{1,0:T(8,128)} %own.1) | copy-start | bytes 1572868
  70.5 5.9 %collective-permute-start.7 = (f32[32,24,128]{2,1,0:T(8,128)S(1)}, f32[32,24,128]{2,1,0:T(8,128)S(1)}, u32[]{:S(2)}, u32[]{:S(2)}) collective-permute-start(f32[32,24,128]{2,1,0:T(8,128)S(1)} %all_to_all.11.mine), channel_id=1, source_target_pairs={{0,4},{4,0},{8,12},{12,8},{16,20},{20,16},{24,28},{28,24},{32,36},... | collective-permute-start | bytes 1179656 | tf_op jit(solution)/shard_map/ppermute | solution.py:230

commit v4 on v3

--- a/solution.py
+++ b/solution.py
@@ -4,6 +4,7 @@
 from jax.experimental import pallas as pl
 from jax.experimental.pallas import tpu as pltpu
 from jax.sharding import PartitionSpec as P
+
 
 NY, NZ, NC, NX = 4, 8, 2, 4
 HIGHEST = lax.Precision.HIGHEST
@@ -114,10 +115,29 @@
     return jax.ShapeDtypeStruct(shape, F32)
 
 
+def gram_kernel(core, panel, mine, other, whole):
+    a = panel[...]
+    whole[...] = dot(a.T, a)
+    m, o = starts([core[0]])
+    cut(whole, m, mine, 0)
+    cut(whole, o, other, 0)
+
+
+def gram_of(core, panel):
+    return pl.pallas_call(
+        gram_kernel,
+        out_shape=(shaped(32, 8, 128), shaped(32, 8, 128)),
+        in_specs=[SCALARS, VMEM],
+        scratch_shapes=[pltpu.VMEM((256, 256), F32)],
+        compiler_params=SMALL,
+        name="gram",
+    )(core, panel)
+
+
 def factor_kernel(core, mine, other, r, x, gram):
     m, o = starts([core[0]])
     paste(mine, m, gram, 16)
-    paste(other, o, gram, 16)
+    paste(other, o, gram, 0)
     r00, x00 = factor_block(gram[:128, :128])
     r01 = dot(x00, gram[:128, 128:])
     r01t = r01.T
@@ -146,40 +166,32 @@
 
 
 def accumulate(pieces, trails):
-    cross, gram = 0.0, 0.0
+    total = 0.0
     for piece, trail in zip(pieces, trails):
-        flipped, straight = split(piece.T), split(piece)
-        cross = cross + product(flipped, split(trail))
-        gram = gram + (product(flipped, straight) + dot(flipped[1], straight[1], precision=None))
-    return cross, gram
+        total = total + product(split(piece.T), split(trail))
+    return total
 
 
 def rows_at(ref, place, first=0, n=512):
     return ref[pl.ds(pl.multiple_of(place * 512 + first, 256), n), :]
 
 
-def cross_own(places, panel, trailing, keep, cross, gram):
-    keep[...] = trailing[...]
-    cross[...], gram[...] = accumulate([panel[...]], [rows_at(trailing, places[0])])
-
-
-def cross_near(places, b1, b2, a1, a2, keep, cross0, gram0, cross, gram):
-    trails = [rows_at(keep, places[k], first, 256) for k in (1, 2) for first in (0, 256)]
-    c, g = accumulate([b1[...], b2[...], a1[...], a2[...]], trails)
-    cross[...] = cross0[...] + c
-    gram[...] = gram0[...] + g
-
-
-def cross_far(places, f1, f2, keep, cross0, gram0, mine, other, cross, gram):
-    trails = [rows_at(keep, places[3], first, 256) for first in (0, 256)]
-    c, g = accumulate([f1[...], f2[...]], trails)
-    cross[...] = cross0[...] + c
-    gram[...] = gram0[...] + g
+def cross_near(places, own, b1, b2, a1, a2, trailing, hi, lo, cross):
+    trails = [rows_at(trailing, places[k], first, 256) for k in (1, 2) for first in (0, 256)]
+    trails.insert(0, rows_at(trailing, places[0]))
+    cross[...] = accumulate([own[...], b1[...], b2[...], a1[...], a2[...]], trails)
+    hi[...], lo[...] = split(rows_at(trailing, places[3]))
+
+
+def cross_far(places, f1, f2, hi, lo, cross0, mine, other, cross):
+    total = cross0[...]
+    for i, part in enumerate((f1, f2)):
+        rows = slice(256 * i, 256 * i + 256)
+        total = total + product(split(part[...].T), (hi[rows, :], lo[rows, :]))
+    cross[...] = total
     m, o = starts([places[4]])
     cut(cross, m, mine, 0)
-    cut(gram, m, mine, 16)
     cut(cross, o, other, 0)
-    cut(gram, o, other, 16)
 
 
 def call(kernel, places, arrays, outs, flops, scratch=()):
@@ -191,17 +203,21 @@
         scratch_shapes=scratch,
         compiler_params=SMALL,
         cost_estimate=pl.CostEstimate(flops=flops, bytes_accessed=2**21, transcendentals=0),
-        name=kernel.__name__,
     )(places, *arrays)
 
 
-def finish(places, inverse, mine, other, own, b1, b2, a1, a2, f1, f2, trailing, projected, updated, cross, result, writes):
+def weights(places, inverse, mine, other, projected, hi, lo, cross):
     m, o = starts([places[4]])
     paste(mine, m, cross, 0)
     paste(other, o, cross, 0)
-    p = dot(inverse[...], cross[...])
+    x = inverse[...]
+    p = product(split(x), split(cross[...]))
     projected[...] = p
-    w = split(dot(inverse[...], p, ((0,), (0,))))
+    hi[...], lo[...] = split(product(split(x.T), split(p)))
+
+
+def update(places, hi, lo, own, b1, b2, a1, a2, f1, f2, trailing, updated, result, writes):
+    w = hi[...], lo[...]
     moves = []
     for k, parts in enumerate([(own,), (b1, b2), (a1, a2), (f1, f2)]):
         n = 512 // len(parts)
@@ -214,15 +230,15 @@
         move.wait()
 
 
-def finished(places, arrays):
-    return pl.pallas_call(
-        finish,
+def updated_of(places, arrays):
+    return pl.pallas_call(
+        update,
         in_specs=[SCALARS] + [VMEM] * len(arrays),
-        out_specs=[VMEM, pl.BlockSpec(memory_space=pltpu.HBM)],
-        out_shape=[shaped(256, 512), shaped(2048, 512)],
-        scratch_shapes=[pltpu.VMEM((256, 512), F32), pltpu.VMEM((4, 512, 512), F32), pltpu.SemaphoreType.DMA((4,))],
-        compiler_params=SMALL,
-        name="finish",
+        out_specs=pl.BlockSpec(memory_space=pltpu.HBM),
+        out_shape=shaped(2048, 512),
+        scratch_shapes=[pltpu.VMEM((4, 512, 512), F32), pltpu.SemaphoreType.DMA((4,))],
+        compiler_params=SMALL,
+        name="update",
     )(places, *arrays)
 
 
@@ -245,25 +261,34 @@
     a2 = shift(low, X_DOWN)
     b2 = shift(low, X_UP)
     a1 = shift(top, X_DOWN)
-    sums = [shaped(256, 512), shaped(256, 256)]
-    keep, *part = call(cross_own, places, [panel, trailing], [shaped(2048, 512), *sums], 10**9)
-    b1, a2, keep, *part = lax.optimization_barrier((b1, a2, keep, *part))
+    mine, other = gram_of(core_word, panel)
+    g = mine + swap(other)
+    g = exchange(g, "rows", GROUP_YZ)
+    g = g.sum(0)
     f1 = shift(b1, X_UP)
     f2 = shift(a2, X_DOWN)
-    part = call(cross_near, places, [b1, b2, a1, a2, keep, *part], sums, 10**8)
-    halves = [shaped(32, 24, 128)] * 2
-    scratch = [pltpu.VMEM((256, 512), F32), pltpu.VMEM((256, 256), F32)]
-    mine, other = call(cross_far, places, [f1, f2, keep, *part], halves, 10**8, scratch)
-    total = exchange(mine + swap(other), "rows", GROUP_YZ).sum(0)
-    mine = exchange(copies(total, 32), "rows", GROUP_YZ)
+    g = exchange(copies(g, 4), "cols")
+    half = jax.ShapeDtypeStruct((512, 512), jnp.bfloat16)
+    part = call(cross_near, places, [panel, b1, b2, a1, a2, trailing], [half, half, shaped(256, 512)], 10**9)
+    g = g.sum(0)
+    halves = [shaped(32, 16, 128)] * 2
+    scratch = [pltpu.VMEM((256, 512), F32)]
+    mine, other = call(cross_far, places, [f1, f2, *part], halves, 10**8, scratch)
+    both = exchange(jnp.concatenate([mine + swap(other), copies(g, 32)], axis=1), "rows", GROUP_YZ)
+    mine = exchange(copies(both[:, :16].sum(0), 32), "rows", GROUP_YZ)
+    rfactor, inverse = factor(core_word, both, swap(both[:, 16:]))
+    inverse, mine = lax.optimization_barrier((inverse, mine))
     other = swap(mine)
-    rfactor, inverse = factor(core_word, mine, other)
-    projected, updated = finished(places, [inverse, mine, other, panel, b1, b2, a1, a2, f1, f2, trailing])
+    small = jax.ShapeDtypeStruct((256, 512), jnp.bfloat16)
+    outs = [shaped(256, 512), small, small]
+    projected, hi, lo = call(weights, places, [inverse, mine, other], outs, FLOPS, [pltpu.VMEM((256, 512), F32)])
+    updated = updated_of(places, [hi, lo, panel, b1, b2, a1, a2, f1, f2, trailing])
     return rfactor, projected, updated
 
 
 def solution(mesh):
     placed = (P(("rows", "cols"), None), P("rows", "cols"))
+
     return jax.shard_map(
         shards,
         mesh=mesh,

time: 91 us -> 95.9 us (1.054)
  starting transfers between devices: 15.2 us -> 35.8 us
  blocking collectives: 41.1 us -> 26.5 us
  waiting for transfers between devices: 9.44 us -> 7.01 us
  local copies, waits for them, and re-layouts: 4.42 us -> 6.17 us
  Pallas kernels: 19.6 us -> 18.2 us
    all_to_all x0 -> x2, starting transfers between devices: none -> 18.5 us  [exchange(): return lax.all_to_all(a, axis, 0, 0, axis_index_groups=groups, tiled=True)]
    all_to_all x2, blocking collectives: 41.1 us -> 26.5 us  [exchange(): return lax.all_to_all(a, axis, 0, 0, axis_index_groups=groups, tiled=True)]
    ppermute x6, waiting for transfers between devices: 6.74 us -> 2.3 us  [shift(): return lax.ppermute(a, 'cols', way)]
    all_to_all x0 -> x2, waiting for transfers between devices: none -> 1.65 us  [exchange(): return lax.all_to_all(a, axis, 0, 0, axis_index_groups=groups, tiled=True)]
    ppermute x2 -> x4, starting transfers between devices: 6.43 us -> 7.83 us  [swap(): return lax.ppermute(a, 'rows', CORE_SWAP)]
    pallas_call x1 -> x2, Pallas kernels: 5.39 us -> 4.13 us  [the longest x1 3.38 us: updated_of(): pl.pallas_call(update, in_specs=[SCALARS] + [VMEM] * len(arrays), out_spe...]
    unnamed x8 -> x10, local copies, waits for them, and re-layouts: 3.24 us -> 4.27 us
    ppermute x2 -> x4, waiting for transfers between devices: 2.7 us -> 3.05 us  [swap(): return lax.ppermute(a, 'rows', CORE_SWAP)]
  transfers between devices with their start and end apart: 8 -> 12, of which waited for: 5 -> 5; matrix products, arithmetic and copies ran while one was open for 0% -> 1% of each run, Pallas kernels for 4% -> 14%
where the time goes in v4:
time: 95.9 us; the launch traced here: 95.4 us
  starting transfers between devices  35.8 us (37%)
  blocking collectives  26.5 us (28%)
  Pallas kernels  18.2 us (19%)
  waiting for transfers between devices  7.01 us (7%)
  local copies, waits for them, and re-layouts  6.17 us (6%)
    all_to_all x2, blocking collectives, exchange(): return lax.all_to_all(a, axis, 0, 0, axis_index_groups=groups, tiled=True)  26.5 us
    all_to_all x2, starting transfers between devices, exchange(): return lax.all_to_all(a, axis, 0, 0, axis_index_groups=groups, tiled=True)  18.5 us
    ppermute x6, starting transfers between devices, shift(): return lax.ppermute(a, 'cols', way)  9.48 us
    pallas_call x1, Pallas kernels, factor(): pl.pallas_call(factor_kernel, out_shape=(shaped(256, 256), shaped(256, 25...  8.8 us
    ppermute x4, starting transfers between devices, swap(): return lax.ppermute(a, 'rows', CORE_SWAP)  7.83 us
    pallas_call x3, Pallas kernels, call(): pl.pallas_call(kernel, in_specs=[SCALARS] + [VMEM] * len(arrays), out_spe...  5.26 us
    unnamed x10, local copies, waits for them, and re-layouts  4.27 us
    pallas_call x1, Pallas kernels, updated_of(): pl.pallas_call(update, in_specs=[SCALARS] + [VMEM] * len(arrays), out_spe...  3.38 us
  transfers between devices with their start and end apart: 12, of which 5 were waited for; matrix products, arithmetic and copies ran while one was open for 1% of the time, Pallas kernels for 14%

profile of v4, /device:TPU:1, one launch (start us, length us, event | category | flops | bytes accessed | tf_op | source)
XLA Modules:
  0.0 95.4 jit_solution(11582236833567511309)
XLA Ops:
  0.6 1.1 %fusion = (f32[256,256]{1,0:T(8,128)S(1)}, f32[256,256]{1,0:T(8,128)S(1)}) fusion(f32[512,256]{1,0:T(8,128)} %own.3), kind=kLoop, calls=%fused_computation.2 | loop fusion | bytes 1048576 | tf_op jit(solution)/shard_map/slice | solution.py:259
  1.7 3.4 %collective-permute-start.2 = (f32[256,256]{1,0:T(8,128)S(1)}, f32[256,256]{1,0:T(8,128)S(1)}, u32[]{:S(2)}, u32[]{:S(2)}) collective-permute-start(f32[256,256]{1,0:T(8,128)S(1)} %get-tuple-element.31), channel_id=1, source_target_pairs={{0,3},{1,0},{2,1},{3,2},{4,7},{5,4},{6,5},{7,6},{8,11},{9,8},{10,9... | collective-permute-start | bytes 786440 | tf_op jit(solution)/shard_map/ppermute | solution.py:250
  5.1 0.0 collective-permute-start
  5.1 0.2 collective-permute-start.4
  5.3 2.5 %collective-permute-start.5 = (f32[256,256]{1,0:T(8,128)S(1)}, f32[256,256]{1,0:T(8,128)S(1)}, u32[]{:S(2)}, u32[]{:S(2)}) collective-permute-start(f32[256,256]{1,0:T(8,128)S(1)} %get-tuple-element.32), channel_id=1, source_target_pairs={{0,3},{1,0},{2,1},{3,2},{4,7},{5,4},{6,5},{7,6},{8,11},{9,8},{10,9... | collective-permute-start | bytes 786440 | tf_op jit(solution)/shard_map/ppermute | solution.py:250
  7.8 2.3 %collective-permute-done.2.a2 = f32[256,256]{1,0:T(8,128)S(1)} collective-permute-done((f32[256,256]{1,0:T(8,128)S(1)}, f32[256,256]{1,0:T(8,128)S(1)}, u32[]{:S(2)}, u32[]{:S(2)}) %collective-permute-start.2) | collective-permute-done | bytes 262176 | tf_op jit(solution)/shard_map/ppermute | solution.py:250
  10.1 3.4 %collective-permute-start.3 = (f32[256,256]{1,0:T(8,128)S(1)}, f32[256,256]{1,0:T(8,128)S(1)}, u32[]{:S(2)}, u32[]{:S(2)}) collective-permute-start(f32[256,256]{1,0:T(8,128)S(1)} %collective-permute-done.2.a2), channel_id=1, source_target_pairs={{0,3},{1,0},{2,1},{3,2},{4,7},{5,4},{6,5},{7,6},{8,11},{9,8},{10,9... | collective-permute-start | bytes 786440 | tf_op jit(solution)/shard_map/ppermute | solution.py:250
  13.5 0.0 collective-permute-done.b1
  13.5 0.0 collective-permute-start.1
  13.5 0.0 copy-start.2
  13.5 1.0 %copy-done.2 = f32[512,256]{1,0:T(8,128)S(1)} copy-done((f32[512,256]{1,0:T(8,128)S(1)}, f32[512,256]{1,0:T(8,128)}, u32[]{:S(2)}) %copy-start.2) | copy-done | bytes 524312
  14.5 0.7 gram.1
  15.3 3.0 %collective-permute-start.7 = (f32[32,8,128]{2,1,0:T(8,128)S(1)}, f32[32,8,128]{2,1,0:T(8,128)S(1)}, u32[]{:S(2)}, u32[]{:S(2)}) collective-permute-start(f32[32,8,128]{2,1,0:T(8,128)S(1)} %get-tuple-element.23), channel_id=1, source_target_pairs={{0,4},{4,0},{8,12},{12,8},{16,20},{20,16},{24,28},{28,24},{32,36},... | collective-permute-start | bytes 393224 | tf_op jit(solution)/shard_map/ppermute | solution.py:246
  18.3 0.1 stack.20.places
  18.4 0.9 collective-permute-done.7
  19.3 0.7 add.36
  20.0 11.2 %all-to-all-start = ((f32[32,8,128]{2,1,0:T(8,128)}), f32[32,8,128]{2,1,0:T(8,128)S(1)}, u32[]{:S(2)}, u32[]{:S(2)}) async-start(f32[32,8,128]{2,1,0:T(8,128)} %add.36), calls=%async_computation | async-start | bytes 262144 | tf_op jit(solution)/shard_map/all_to_all | solution.py:29
  31.2 0.0 collective-permute-done.4.b2
  31.2 0.0 collective-permute-done.5.a1
  31.2 0.0 copy-start
  31.2 2.2 %copy-done = f32[2048,512]{1,0:T(8,128)S(1)} copy-done((f32[2048,512]{1,0:T(8,128)S(1)}, f32[2048,512]{1,0:T(8,128)}, u32[]{:S(2)}) %copy-start) | copy-done | bytes 4194328
  33.4 0.0 copy-start.3
  33.4 1.0 %copy-done.3 = f32[512,256]{1,0:T(8,128)S(1)} copy-done((f32[512,256]{1,0:T(8,128)S(1)}, f32[512,256]{1,0:T(8,128)}, u32[]{:S(2)}) %copy-start.3) | copy-done | bytes 524312
  34.4 2.3 %shard_map.49 = (bf16[512,512]{1,0:T(8,128)(2,1)S(1)}, bf16[512,512]{1,0:T(8,128)(2,1)S(1)}, f32[256,512]{1,0:T(8,128)S(1)}) custom-call(s32[5]{0:T(128)S(1)} %stack.20.places, f32[512,256]{1,0:T(8,128)S(1)} %copy-done.3, f32[256,256]{1,0:T(8,128)S(1)} %collective-permute-done.b1, f32[256,256]{1,0:T(8,128)S(1)} %collective-permute-done.4.b2, ...), custom_call_target="tpu_custom_call" | custom-call | flops 1000000000 | bytes 2097152 | tf_op jit(solution)/shard_map/pallas_call | solution.py:198
  36.7 0.0 collective-permute-done.3.f2
  36.7 0.0 collective-permute-done.1.f1
  36.7 1.2 %shard_map.50 = (f32[32,16,128]{2,1,0:T(8,128)S(1)}, f32[32,16,128]{2,1,0:T(8,128)S(1)}) custom-call(s32[5]{0:T(128)S(1)} %stack.20.places, f32[256,256]{1,0:T(8,128)S(1)} %collective-permute-done.1.f1, f32[256,256]{1,0:T(8,128)S(1)} %collective-permute-done.3.f2, bf16[512,512]{1,0:T(8,128)(2,1)S(1)} %get-tuple-element.17.hi, ...), custom_call_target="tpu_custom_call" | custom-call | flops 100000000 | bytes 2097152 | tf_op jit(solution)/shard_map/pallas_call | solution.py:198
  38.0 0.7 collective-permute-start.6
  38.7 1.6 %all-to-all-done = f32[32,8,128]{2,1,0:T(8,128)S(1)} async-done(((f32[32,8,128]{2,1,0:T(8,128)}), f32[32,8,128]{2,1,0:T(8,128)S(1)}, u32[]{:S(2)}, u32[]{:S(2)}) %all-to-all-start) | async-done | bytes 131104 | tf_op jit(solution)/shard_map/all_to_all | solution.py:29
  40.4 8.2 %all_to_all.20 = f32[4,8,128]{2,1,0:T(8,128)S(1)} all-to-all(f32[4,8,128]{2,1,0:T(8,128)S(1)} %broadcast_in_dim.6), channel_id=1, replica_groups=mesh['rows'=64,'cols'=4] {'cols'}, dimensions={0} | all-to-all | bytes 32768 | tf_op jit(solution)/shard_map/all_to_all | solution.py:29
  48.6 0.0 collective-permute-done.6
  48.7 18.2 %all_to_all.21.mine = f32[32,24,128]{2,1,0:T(8,128)S(1)} all-to-all(f32[32,24,128]{2,1,0:T(8,128)S(1)} %pad_maximum_fusion), channel_id=1, replica_groups={{0,8,16,24,32,40,48,56,64,72,80,88,96,104,112,120,128,136,144,152,160,1..., dimensions={0} | all-to-all | bytes 786432 | tf_op jit(solution)/shard_map/all_to_all | solution.py:29
  67.0 0.7 broadcast_in_dim.8
  67.7 7.3 %all-to-all-start.3 = ((f32[32,16,128]{2,1,0:T(8,128)}), f32[32,16,128]{2,1,0:T(8,128)S(1)}, u32[]{:S(2)}, u32[]{:S(2)}) async-start(f32[32,16,128]{2,1,0:T(8,128)} %broadcast_in_dim.8), calls=%async_computation.3 | async-start | bytes 524288 | tf_op jit(solution)/shard_map/all_to_all | solution.py:29
  75.0 3.0 %collective-permute-start.8 = (f32[32,8,128]{2,1,0:T(8,128)S(1)}, f32[32,8,128]{2,1,0:T(8,128)S(1)}, u32[]{:S(2)}, u32[]{:S(2)}) collective-permute-start(f32[32,8,128]{2,1,0:T(8,128)S(1)} %slice.16), channel_id=1, source_target_pairs={{0,4},{4,0},{8,12},{12,8},{16,20},{20,16},{24,28},{28,24},{32,36},... | collective-permute-start | bytes 393224 | tf_op jit(solution)/shard_map/ppermute | solution.py:246
  78.0 1.0 %collective-permute-done.8.other = f32[32,8,128]{2,1,0:T(8,128)S(1)} collective-permute-done((f32[32,8,128]{2,1,0:T(8,128)S(1)}, f32[32,8,128]{2,1,0:T(8,128)S(1)}, u32[]{:S(2)}, u32[]{:S(2)}) %collective-permute-start.8) | collective-permute-done | bytes 131104 | tf_op jit(solution)/shard_map/ppermute | solution.py:246
  79.0 8.8 %factor.1 = (f32[256,256]{1,0:T(8,128)}, f32[256,256]{1,0:T(8,128)S(1)}) custom-call(s32[1]{0:T(128)} %bitcast.core, f32[32,24,128]{2,1,0:T(8,128)S(1)} %all_to_all.21.mine, f32[32,8,128]{2,1,0:T(8,128)S(1)} %collective-permute-done.8.other), custom_call_target="tpu_custom_call" | custom-call | flops 4000000000 | bytes 1048576 | tf_op jit(solution)/shard_map/factor/pallas_call | solution.py:157
  87.8 0.0 all-to-all-done.3.mine
  87.8 0.0 copy-start.1
  87.8 0.0 copy-start.4
  87.8 1.1 %collective-permute-start.9 = (f32[32,16,128]{2,1,0:T(8,128)S(1)}, f32[32,16,128]{2,1,0:T(8,128)S(1)}, u32[]{:S(2)}, u32[]{:S(2)}) collective-permute-start(f32[32,16,128]{2,1,0:T(8,128)S(1)} %all-to-all-done.3.mine), channel_id=1, source_target_pairs={{0,4},{4,0},{8,12},{12,8},{16,20},{20,16},{24,28},{28,24},{32,36},... | collective-permute-start | bytes 786440 | tf_op jit(solution)/shard_map/ppermute | solution.py:246
  88.9 1.2 %collective-permute-done.9.other = f32[32,16,128]{2,1,0:T(8,128)S(1)} collective-permute-done((f32[32,16,128]{2,1,0:T(8,128)S(1)}, f32[32,16,128]{2,1,0:T(8,128)S(1)}, u32[]{:S(2)}, u32[]{:S(2)}) %collective-permute-start.9) | collective-permute-done | bytes 262176 | tf_op jit(solution)/shard_map/ppermute | solution.py:246
  90.1 1.8 %shard_map.51 = (f32[256,512]{1,0:T(8,128)}, bf16[256,512]{1,0:T(8,128)(2,1)S(1)}, bf16[256,512]{1,0:T(8,128)(2,1)S(1)}) custom-call(s32[5]{0:T(128)S(1)} %stack.20.places, f32[256,256]{1,0:T(8,128)S(1)} %get-tuple-element.26.inverse, f32[32,16,128]{2,1,0:T(8,128)S(1)} %all-to-all-done.3.mine, f32[32,16,128]{2,1,0:T(8,128)S(1)} %collective-permute-done.9.other), custom_call_target="tpu_custom_call" | custom-call | flops 4000000000 | bytes 2097152 | tf_op jit(solution)/shard_map/pallas_call | solution.py:198
  91.8 0.0 copy-done.1
  91.9 0.0 copy-done.4
  91.9 3.4 %update.1 = f32[2048,512]{1,0:T(8,128)} custom-call(s32[5]{0:T(128)S(1)} %stack.20.places, bf16[256,512]{1,0:T(8,128)(2,1)S(1)} %get-tuple-element.29.hi, bf16[256,512]{1,0:T(8,128)(2,1)S(1)} %get-tuple-element.30.lo, f32[512,256]{1,0:T(8,128)S(1)} %copy-done.4, f32[256,256]{1,0:T(8,128)S(1)} %collective-permute-done.b1, ...), custom_call_target="tpu_custom_call" | custom-call | tf_op jit(solution)/shard_map/update/pallas_call | solution.py:234
  (8 shorter events, 0.2 us)
Async XLA Ops:
  1.7 8.4 %collective-permute-start.2 = (f32[256,256]{1,0:T(8,128)S(1)}, f32[256,256]{1,0:T(8,128)S(1)}, u32[]{:S(2)}, u32[]{:S(2)}) collective-permute-start(f32[256,256]{1,0:T(8,128)S(1)} %get-tuple-element.31), channel_id=1, source_target_pairs={{0,3},{1,0},{2,1},{3,2},{4,7},{5,4},{6,5},{7,6},{8,11},{9,8},{10,9... | collective-permute-start | bytes 786440 | tf_op jit(solution)/shard_map/ppermute | solution.py:250
  5.1 8.4 %collective-permute-start = (f32[256,256]{1,0:T(8,128)S(1)}, f32[256,256]{1,0:T(8,128)S(1)}, u32[]{:S(2)}, u32[]{:S(2)}) collective-permute-start(f32[256,256]{1,0:T(8,128)S(1)} %get-tuple-element.32), channel_id=1, source_target_pairs={{0,1},{1,2},{2,3},{3,0},{4,5},{5,6},{6,7},{7,4},{8,9},{9,10},{10,1... | collective-permute-start | bytes 786440 | tf_op jit(solution)/shard_map/ppermute | solution.py:250
  5.1 26.1 %collective-permute-start.4 = (f32[256,256]{1,0:T(8,128)S(1)}, f32[256,256]{1,0:T(8,128)S(1)}, u32[]{:S(2)}, u32[]{:S(2)}) collective-permute-start(f32[256,256]{1,0:T(8,128)S(1)} %get-tuple-element.31), channel_id=1, source_target_pairs={{0,1},{1,2},{2,3},{3,0},{4,5},{5,6},{6,7},{7,4},{8,9},{9,10},{10,1... | collective-permute-start | bytes 786440 | tf_op jit(solution)/shard_map/ppermute | solution.py:250
  5.3 25.9 %collective-permute-start.5 = (f32[256,256]{1,0:T(8,128)S(1)}, f32[256,256]{1,0:T(8,128)S(1)}, u32[]{:S(2)}, u32[]{:S(2)}) collective-permute-start(f32[256,256]{1,0:T(8,128)S(1)} %get-tuple-element.32), channel_id=1, source_target_pairs={{0,3},{1,0},{2,1},{3,2},{4,7},{5,4},{6,5},{7,6},{8,11},{9,8},{10,9... | collective-permute-start | bytes 786440 | tf_op jit(solution)/shard_map/ppermute | solution.py:250
  10.1 26.6 %collective-permute-start.3 = (f32[256,256]{1,0:T(8,128)S(1)}, f32[256,256]{1,0:T(8,128)S(1)}, u32[]{:S(2)}, u32[]{:S(2)}) collective-permute-start(f32[256,256]{1,0:T(8,128)S(1)} %collective-permute-done.2.a2), channel_id=1, source_target_pairs={{0,3},{1,0},{2,1},{3,2},{4,7},{5,4},{6,5},{7,6},{8,11},{9,8},{10,9... | collective-permute-start | bytes 786440 | tf_op jit(solution)/shard_map/ppermute | solution.py:250
  13.5 23.2 %collective-permute-start.1 = (f32[256,256]{1,0:T(8,128)S(1)}, f32[256,256]{1,0:T(8,128)S(1)}, u32[]{:S(2)}, u32[]{:S(2)}) collective-permute-start(f32[256,256]{1,0:T(8,128)S(1)} %collective-permute-done.b1), channel_id=1, source_target_pairs={{0,1},{1,2},{2,3},{3,0},{4,5},{5,6},{6,7},{7,4},{8,9},{9,10},{10,1... | collective-permute-start | bytes 786440 | tf_op jit(solution)/shard_map/ppermute | solution.py:250
  13.5 1.0 %copy-start.2 = (f32[512,256]{1,0:T(8,128)S(1)}, f32[512,256]{1,0:T(8,128)}, u32[]{:S(2)}) copy-start(f32[512,256]{1,0:T(8,128)} %own.3) | copy-start | bytes 1572868
  15.3 4.0 %collective-permute-start.7 = (f32[32,8,128]{2,1,0:T(8,128)S(1)}, f32[32,8,128]{2,1,0:T(8,128)S(1)}, u32[]{:S(2)}, u32[]{:S(2)}) collective-permute-start(f32[32,8,128]{2,1,0:T(8,128)S(1)} %get-tuple-element.23), channel_id=1, source_target_pairs={{0,4},{4,0},{8,12},{12,8},{16,20},{20,16},{24,28},{28,24},{32,36},... | collective-permute-start | bytes 393224 | tf_op jit(solution)/shard_map/ppermute | solution.py:246
  20.0 20.4 %all-to-all-start = ((f32[32,8,128]{2,1,0:T(8,128)}), f32[32,8,128]{2,1,0:T(8,128)S(1)}, u32[]{:S(2)}, u32[]{:S(2)}) async-start(f32[32,8,128]{2,1,0:T(8,128)} %add.36), calls=%async_computation | async-start | bytes 262144 | tf_op jit(solution)/shard_map/all_to_all | solution.py:29
  31.2 2.2 %copy-start = (f32[2048,512]{1,0:T(8,128)S(1)}, f32[2048,512]{1,0:T(8,128)}, u32[]{:S(2)}) copy-start(f32[2048,512]{1,0:T(8,128)} %trailing.3) | copy-start | bytes 12582916
  33.4 1.0 %copy-start.3 = (f32[512,256]{1,0:T(8,128)S(1)}, f32[512,256]{1,0:T(8,128)}, u32[]{:S(2)}) copy-start(f32[512,256]{1,0:T(8,128)} %own.3) | copy-start | bytes 1572868
  38.0 10.7 %collective-permute-start.6 = (f32[32,16,128]{2,1,0:T(8,128)S(1)}, f32[32,16,128]{2,1,0:T(8,128)S(1)}, u32[]{:S(2)}, u32[]{:S(2)}) collective-permute-start(f32[32,16,128]{2,1,0:T(8,128)S(1)} %get-tuple-element.21), channel_id=1, source_target_pairs={{0,4},{4,0},{8,12},{12,8},{16,20},{20,16},{24,28},{28,24},{32,36},... | collective-permute-start | bytes 786440 | tf_op jit(solution)/shard_map/ppermute | solution.py:246
  67.7 20.1 %all-to-all-start.3 = ((f32[32,16,128]{2,1,0:T(8,128)}), f32[32,16,128]{2,1,0:T(8,128)S(1)}, u32[]{:S(2)}, u32[]{:S(2)}) async-start(f32[32,16,128]{2,1,0:T(8,128)} %broadcast_in_dim.8), calls=%async_computation.3 | async-start | bytes 524288 | tf_op jit(solution)/shard_map/all_to_all | solution.py:29
  75.0 4.0 %collective-permute-start.8 = (f32[32,8,128]{2,1,0:T(8,128)S(1)}, f32[32,8,128]{2,1,0:T(8,128)S(1)}, u32[]{:S(2)}, u32[]{:S(2)}) collective-permute-start(f32[32,8,128]{2,1,0:T(8,128)S(1)} %slice.16), channel_id=1, source_target_pairs={{0,4},{4,0},{8,12},{12,8},{16,20},{20,16},{24,28},{28,24},{32,36},... | collective-permute-start | bytes 393224 | tf_op jit(solution)/shard_map/ppermute | solution.py:246
  87.8 4.0 %copy-start.1 = (f32[2048,512]{1,0:T(8,128)S(1)}, f32[2048,512]{1,0:T(8,128)}, u32[]{:S(2)}) copy-start(f32[2048,512]{1,0:T(8,128)} %trailing.3) | copy-start | bytes 12582916
  87.8 4.0 %copy-start.4 = (f32[512,256]{1,0:T(8,128)S(1)}, f32[512,256]{1,0:T(8,128)}, u32[]{:S(2)}) copy-start(f32[512,256]{1,0:T(8,128)} %own.3) | copy-start | bytes 1572868
  87.8 2.2 %collective-permute-start.9 = (f32[32,16,128]{2,1,0:T(8,128)S(1)}, f32[32,16,128]{2,1,0:T(8,128)S(1)}, u32[]{:S(2)}, u32[]{:S(2)}) collective-permute-start(f32[32,16,128]{2,1,0:T(8,128)S(1)} %all-to-all-done.3.mine), channel_id=1, source_target_pairs={{0,4},{4,0},{8,12},{12,8},{16,20},{20,16},{24,28},{28,24},{32,36},... | collective-permute-start | bytes 786440 | tf_op jit(solution)/shard_map/ppermute | solution.py:246

commit v5 on v4

--- a/solution.py
+++ b/solution.py
@@ -18,6 +18,7 @@
 GROUP_YZ = [[row_id(y, z, c) for y in range(NY) for z in range(NZ)] for c in range(NC)]
 CORE_SWAP = [(i, i ^ 1) for i in range(NY * NZ * NC)]
 X_UP = [(i, (i + 1) % NX) for i in range(NX)]
+X_ACROSS = [(i, (i + 2) % NX) for i in range(NX)]
 X_DOWN = [(i, (i - 1) % NX) for i in range(NX)]
 
 
@@ -267,10 +268,10 @@
     g = g.sum(0)
     f1 = shift(b1, X_UP)
     f2 = shift(a2, X_DOWN)
-    g = exchange(copies(g, 4), "cols")
+    g1, g2, g3 = shift(g, X_UP), shift(g, X_DOWN), shift(g, X_ACROSS)
     half = jax.ShapeDtypeStruct((512, 512), jnp.bfloat16)
     part = call(cross_near, places, [panel, b1, b2, a1, a2, trailing], [half, half, shaped(256, 512)], 10**9)
-    g = g.sum(0)
+    g = (g + g3) + (g1 + g2)
     halves = [shaped(32, 16, 128)] * 2
     scratch = [pltpu.VMEM((256, 512), F32)]
     mine, other = call(cross_far, places, [f1, f2, *part], halves, 10**8, scratch)

time: 95.9 us -> 91.4 us (0.953)
  blocking collectives: 26.5 us -> 19.9 us
  starting transfers between devices: 35.8 us -> 40.2 us
  waiting for transfers between devices: 7.01 us -> 4.86 us
    all_to_all x2 -> x1, blocking collectives: 26.5 us -> 19.9 us  [exchange(): return lax.all_to_all(a, axis, 0, 0, axis_index_groups=groups, tiled=True)]
    ppermute x6 -> x9, starting transfers between devices: 9.48 us -> 11.8 us  [shift(): return lax.ppermute(a, 'cols', way)]
    ppermute x4, starting transfers between devices: 7.83 us -> 9.94 us  [swap(): return lax.ppermute(a, 'rows', CORE_SWAP)]
    all_to_all x2, waiting for transfers between devices: 1.65 us -> 0.01 us  [exchange(): return lax.all_to_all(a, axis, 0, 0, axis_index_groups=groups, tiled=True)]
    ppermute x6 -> x9, waiting for transfers between devices: 2.3 us -> 2.71 us  [shift(): return lax.ppermute(a, 'cols', way)]
  transfers between devices with their start and end apart: 12 -> 15, of which waited for: 5 -> 4; matrix products, arithmetic and copies ran while one was open for 1% -> 1% of each run, Pallas kernels for 14% -> 14%
where the time goes in v5:
time: 91.4 us; the launch traced here: 91 us
  starting transfers between devices  40.2 us (44%)
  blocking collectives  19.9 us (22%)
  Pallas kernels  18.2 us (20%)
  local copies, waits for them, and re-layouts  6.17 us (7%)
  waiting for transfers between devices  4.86 us (5%)
  between operations  0.94 us (1%)
    all_to_all x1, blocking collectives, exchange(): return lax.all_to_all(a, axis, 0, 0, axis_index_groups=groups, tiled=True)  19.9 us
    all_to_all x2, starting transfers between devices, exchange(): return lax.all_to_all(a, axis, 0, 0, axis_index_groups=groups, tiled=True)  18.4 us
    ppermute x9, starting transfers between devices, shift(): return lax.ppermute(a, 'cols', way)  11.8 us
    ppermute x4, starting transfers between devices, swap(): return lax.ppermute(a, 'rows', CORE_SWAP)  9.94 us
    pallas_call x1, Pallas kernels, factor(): pl.pallas_call(factor_kernel, out_shape=(shaped(256, 256), shaped(256, 25...  8.8 us
    pallas_call x3, Pallas kernels, call(): pl.pallas_call(kernel, in_specs=[SCALARS] + [VMEM] * len(arrays), out_spe...  5.26 us
    unnamed x10, local copies, waits for them, and re-layouts  4.27 us
    pallas_call x1, Pallas kernels, updated_of(): pl.pallas_call(update, in_specs=[SCALARS] + [VMEM] * len(arrays), out_spe...  3.38 us
  transfers between devices with their start and end apart: 15, of which 4 were waited for; matrix products, arithmetic and copies ran while one was open for 1% of the time, Pallas kernels for 14%

profile of v5, /device:TPU:1, one launch (start us, length us, event | category | flops | bytes accessed | tf_op | source)
XLA Modules:
  0.0 91.0 jit_solution(11705009717703629615)
XLA Ops:
  0.6 1.1 %fusion = (f32[256,256]{1,0:T(8,128)S(1)}, f32[256,256]{1,0:T(8,128)S(1)}) fusion(f32[512,256]{1,0:T(8,128)} %own.3), kind=kLoop, calls=%fused_computation.3 | loop fusion | bytes 1048576 | tf_op jit(solution)/shard_map/slice | solution.py:260
  1.7 3.4 %collective-permute-start.2 = (f32[256,256]{1,0:T(8,128)S(1)}, f32[256,256]{1,0:T(8,128)S(1)}, u32[]{:S(2)}, u32[]{:S(2)}) collective-permute-start(f32[256,256]{1,0:T(8,128)S(1)} %get-tuple-element.31), channel_id=1, source_target_pairs={{0,3},{1,0},{2,1},{3,2},{4,7},{5,4},{6,5},{7,6},{8,11},{9,8},{10,9... | collective-permute-start | bytes 786440 | tf_op jit(solution)/shard_map/ppermute | solution.py:251
  5.1 0.0 collective-permute-start
  5.1 0.2 collective-permute-start.4
  5.3 2.5 %collective-permute-start.5 = (f32[256,256]{1,0:T(8,128)S(1)}, f32[256,256]{1,0:T(8,128)S(1)}, u32[]{:S(2)}, u32[]{:S(2)}) collective-permute-start(f32[256,256]{1,0:T(8,128)S(1)} %get-tuple-element.32), channel_id=1, source_target_pairs={{0,3},{1,0},{2,1},{3,2},{4,7},{5,4},{6,5},{7,6},{8,11},{9,8},{10,9... | collective-permute-start | bytes 786440 | tf_op jit(solution)/shard_map/ppermute | solution.py:251
  7.8 0.0 copy-start.2
  7.8 1.0 %copy-done.2 = f32[512,256]{1,0:T(8,128)S(1)} copy-done((f32[512,256]{1,0:T(8,128)S(1)}, f32[512,256]{1,0:T(8,128)}, u32[]{:S(2)}) %copy-start.2) | copy-done | bytes 524312
  8.8 0.7 gram.1
  9.6 2.6 %collective-permute-start.7 = (f32[32,8,128]{2,1,0:T(8,128)S(1)}, f32[32,8,128]{2,1,0:T(8,128)S(1)}, u32[]{:S(2)}, u32[]{:S(2)}) collective-permute-start(f32[32,8,128]{2,1,0:T(8,128)S(1)} %get-tuple-element.23), channel_id=1, source_target_pairs={{0,4},{4,0},{8,12},{12,8},{16,20},{20,16},{24,28},{28,24},{32,36},... | collective-permute-start | bytes 393224 | tf_op jit(solution)/shard_map/ppermute | solution.py:247
  12.1 0.0 collective-permute-done.2.a2
  12.1 1.4 %collective-permute-start.3 = (f32[256,256]{1,0:T(8,128)S(1)}, f32[256,256]{1,0:T(8,128)S(1)}, u32[]{:S(2)}, u32[]{:S(2)}) collective-permute-start(f32[256,256]{1,0:T(8,128)S(1)} %collective-permute-done.2.a2), channel_id=1, source_target_pairs={{0,3},{1,0},{2,1},{3,2},{4,7},{5,4},{6,5},{7,6},{8,11},{9,8},{10,9... | collective-permute-start | bytes 786440 | tf_op jit(solution)/shard_map/ppermute | solution.py:251
  13.5 0.0 collective-permute-done.b1
  13.5 0.1 collective-permute-start.1
  13.6 0.0 collective-permute-done.7
  13.6 0.7 add.45
  14.3 11.1 %all-to-all-start = ((f32[32,8,128]{2,1,0:T(8,128)}), f32[32,8,128]{2,1,0:T(8,128)S(1)}, u32[]{:S(2)}, u32[]{:S(2)}) async-start(f32[32,8,128]{2,1,0:T(8,128)} %add.45), calls=%async_computation | async-start | bytes 262144 | tf_op jit(solution)/shard_map/all_to_all | solution.py:30
  25.4 0.1 stack.20.places
  25.5 0.0 collective-permute-done.4.b2
  25.5 0.0 collective-permute-done.5.a1
  25.5 0.0 copy-start
  25.5 2.2 %copy-done = f32[2048,512]{1,0:T(8,128)S(1)} copy-done((f32[2048,512]{1,0:T(8,128)S(1)}, f32[2048,512]{1,0:T(8,128)}, u32[]{:S(2)}) %copy-start) | copy-done | bytes 4194328
  27.7 0.0 copy-start.3
  27.7 1.0 %copy-done.3 = f32[512,256]{1,0:T(8,128)S(1)} copy-done((f32[512,256]{1,0:T(8,128)S(1)}, f32[512,256]{1,0:T(8,128)}, u32[]{:S(2)}) %copy-start.3) | copy-done | bytes 524312
  28.7 2.3 %shard_map.49 = (bf16[512,512]{1,0:T(8,128)(2,1)S(1)}, bf16[512,512]{1,0:T(8,128)(2,1)S(1)}, f32[256,512]{1,0:T(8,128)S(1)}) custom-call(s32[5]{0:T(128)S(1)} %stack.20.places, f32[512,256]{1,0:T(8,128)S(1)} %copy-done.3, f32[256,256]{1,0:T(8,128)S(1)} %collective-permute-done.b1, f32[256,256]{1,0:T(8,128)S(1)} %collective-permute-done.4.b2, ...), custom_call_target="tpu_custom_call" | custom-call | flops 1000000000 | bytes 2097152 | tf_op jit(solution)/shard_map/pallas_call | solution.py:199
  31.0 0.0 collective-permute-done.3.f2
  31.0 0.0 collective-permute-done.1.f1
  31.0 1.2 %shard_map.50 = (f32[32,16,128]{2,1,0:T(8,128)S(1)}, f32[32,16,128]{2,1,0:T(8,128)S(1)}) custom-call(s32[5]{0:T(128)S(1)} %stack.20.places, f32[256,256]{1,0:T(8,128)S(1)} %collective-permute-done.1.f1, f32[256,256]{1,0:T(8,128)S(1)} %collective-permute-done.3.f2, bf16[512,512]{1,0:T(8,128)(2,1)S(1)} %get-tuple-element.17.hi, ...), custom_call_target="tpu_custom_call" | custom-call | flops 100000000 | bytes 2097152 | tf_op jit(solution)/shard_map/pallas_call | solution.py:199
  32.2 3.3 %collective-permute-start.6 = (f32[32,16,128]{2,1,0:T(8,128)S(1)}, f32[32,16,128]{2,1,0:T(8,128)S(1)}, u32[]{:S(2)}, u32[]{:S(2)}) collective-permute-start(f32[32,16,128]{2,1,0:T(8,128)S(1)} %get-tuple-element.21), channel_id=1, source_target_pairs={{0,4},{4,0},{8,12},{12,8},{16,20},{20,16},{24,28},{28,24},{32,36},... | collective-permute-start | bytes 786440 | tf_op jit(solution)/shard_map/ppermute | solution.py:247
  35.6 0.0 all-to-all-done
  35.6 3.0 %collective-permute-start.10 = (f32[8,128]{1,0:T(8,128)S(1)}, f32[8,128]{1,0:T(8,128)S(1)}, u32[]{:S(2)}, u32[]{:S(2)}) collective-permute-start(f32[8,128]{1,0:T(8,128)S(1)} %reduce_sum.18), channel_id=1, source_target_pairs={{0,3},{1,0},{2,1},{3,2},{4,7},{5,4},{6,5},{7,6},{8,11},{9,8},{10,9... | collective-permute-start | bytes 12296 | tf_op jit(solution)/shard_map/ppermute | solution.py:251
  38.6 0.0 collective-permute-start.9
  38.6 1.3 %collective-permute-start.8 = (f32[8,128]{1,0:T(8,128)S(1)}, f32[8,128]{1,0:T(8,128)S(1)}, u32[]{:S(2)}, u32[]{:S(2)}) collective-permute-start(f32[8,128]{1,0:T(8,128)S(1)} %reduce_sum.18), channel_id=1, source_target_pairs={{0,2},{1,3},{2,0},{3,1},{4,6},{5,7},{6,4},{7,5},{8,10},{9,11},{10,... | collective-permute-start | bytes 12296 | tf_op jit(solution)/shard_map/ppermute | solution.py:251
  39.9 0.0 collective-permute-done.10
  39.9 2.4 %collective-permute-done.9 = f32[8,128]{1,0:T(8,128)S(1)} collective-permute-done((f32[8,128]{1,0:T(8,128)S(1)}, f32[8,128]{1,0:T(8,128)S(1)}, u32[]{:S(2)}, u32[]{:S(2)}) %collective-permute-start.9) | collective-permute-done | bytes 4128 | tf_op jit(solution)/shard_map/ppermute | solution.py:251
  42.3 0.3 collective-permute-done.8
  42.6 0.0 collective-permute-done.6
  42.7 19.9 %all_to_all.15.mine = f32[32,24,128]{2,1,0:T(8,128)S(1)} all-to-all(f32[32,24,128]{2,1,0:T(8,128)S(1)} %pad_maximum_fusion), channel_id=1, replica_groups={{0,8,16,24,32,40,48,56,64,72,80,88,96,104,112,120,128,136,144,152,160,1..., dimensions={0} | all-to-all | bytes 786432 | tf_op jit(solution)/shard_map/all_to_all | solution.py:30
  62.6 0.7 broadcast_in_dim.5
  63.3 7.3 %all-to-all-start.2 = ((f32[32,16,128]{2,1,0:T(8,128)}), f32[32,16,128]{2,1,0:T(8,128)S(1)}, u32[]{:S(2)}, u32[]{:S(2)}) async-start(f32[32,16,128]{2,1,0:T(8,128)} %broadcast_in_dim.5), calls=%async_computation.2 | async-start | bytes 524288 | tf_op jit(solution)/shard_map/all_to_all | solution.py:30
  70.7 3.0 %collective-permute-start.11 = (f32[32,8,128]{2,1,0:T(8,128)S(1)}, f32[32,8,128]{2,1,0:T(8,128)S(1)}, u32[]{:S(2)}, u32[]{:S(2)}) collective-permute-start(f32[32,8,128]{2,1,0:T(8,128)S(1)} %slice.16), channel_id=1, source_target_pairs={{0,4},{4,0},{8,12},{12,8},{16,20},{20,16},{24,28},{28,24},{32,36},... | collective-permute-start | bytes 393224 | tf_op jit(solution)/shard_map/ppermute | solution.py:247
  73.7 1.0 %collective-permute-done.11.other = f32[32,8,128]{2,1,0:T(8,128)S(1)} collective-permute-done((f32[32,8,128]{2,1,0:T(8,128)S(1)}, f32[32,8,128]{2,1,0:T(8,128)S(1)}, u32[]{:S(2)}, u32[]{:S(2)}) %collective-permute-start.11) | collective-permute-done | bytes 131104 | tf_op jit(solution)/shard_map/ppermute | solution.py:247
  74.7 8.8 %factor.1 = (f32[256,256]{1,0:T(8,128)}, f32[256,256]{1,0:T(8,128)S(1)}) custom-call(s32[1]{0:T(128)} %bitcast.core, f32[32,24,128]{2,1,0:T(8,128)S(1)} %all_to_all.15.mine, f32[32,8,128]{2,1,0:T(8,128)S(1)} %collective-permute-done.11.other), custom_call_target="tpu_custom_call" | custom-call | flops 4000000000 | bytes 1048576 | tf_op jit(solution)/shard_map/factor/pallas_call | solution.py:158
  83.5 0.0 all-to-all-done.2.mine
  83.5 0.0 copy-start.1
  83.5 0.0 copy-start.4
  83.5 1.1 %collective-permute-start.12 = (f32[32,16,128]{2,1,0:T(8,128)S(1)}, f32[32,16,128]{2,1,0:T(8,128)S(1)}, u32[]{:S(2)}, u32[]{:S(2)}) collective-permute-start(f32[32,16,128]{2,1,0:T(8,128)S(1)} %all-to-all-done.2.mine), channel_id=1, source_target_pairs={{0,4},{4,0},{8,12},{12,8},{16,20},{20,16},{24,28},{28,24},{32,36},... | collective-permute-start | bytes 786440 | tf_op jit(solution)/shard_map/ppermute | solution.py:247
  84.5 1.2 %collective-permute-done.12.other = f32[32,16,128]{2,1,0:T(8,128)S(1)} collective-permute-done((f32[32,16,128]{2,1,0:T(8,128)S(1)}, f32[32,16,128]{2,1,0:T(8,128)S(1)}, u32[]{:S(2)}, u32[]{:S(2)}) %collective-permute-start.12) | collective-permute-done | bytes 262176 | tf_op jit(solution)/shard_map/ppermute | solution.py:247
  85.7 1.8 %shard_map.51 = (f32[256,512]{1,0:T(8,128)}, bf16[256,512]{1,0:T(8,128)(2,1)S(1)}, bf16[256,512]{1,0:T(8,128)(2,1)S(1)}) custom-call(s32[5]{0:T(128)S(1)} %stack.20.places, f32[256,256]{1,0:T(8,128)S(1)} %get-tuple-element.26.inverse, f32[32,16,128]{2,1,0:T(8,128)S(1)} %all-to-all-done.2.mine, f32[32,16,128]{2,1,0:T(8,128)S(1)} %collective-permute-done.12.other), custom_call_target="tpu_custom_call" | custom-call | flops 4000000000 | bytes 2097152 | tf_op jit(solution)/shard_map/pallas_call | solution.py:199
  87.5 0.0 copy-done.1
  87.5 0.0 copy-done.4
  87.5 3.4 %update.1 = f32[2048,512]{1,0:T(8,128)} custom-call(s32[5]{0:T(128)S(1)} %stack.20.places, bf16[256,512]{1,0:T(8,128)(2,1)S(1)} %get-tuple-element.29.hi, bf16[256,512]{1,0:T(8,128)(2,1)S(1)} %get-tuple-element.30.lo, f32[512,256]{1,0:T(8,128)S(1)} %copy-done.4, f32[256,256]{1,0:T(8,128)S(1)} %collective-permute-done.b1, ...), custom_call_target="tpu_custom_call" | custom-call | tf_op jit(solution)/shard_map/update/pallas_call | solution.py:235
  (7 shorter events, 0.2 us)
Async XLA Ops:
  1.7 10.4 %collective-permute-start.2 = (f32[256,256]{1,0:T(8,128)S(1)}, f32[256,256]{1,0:T(8,128)S(1)}, u32[]{:S(2)}, u32[]{:S(2)}) collective-permute-start(f32[256,256]{1,0:T(8,128)S(1)} %get-tuple-element.31), channel_id=1, source_target_pairs={{0,3},{1,0},{2,1},{3,2},{4,7},{5,4},{6,5},{7,6},{8,11},{9,8},{10,9... | collective-permute-start | bytes 786440 | tf_op jit(solution)/shard_map/ppermute | solution.py:251
  5.1 8.4 %collective-permute-start = (f32[256,256]{1,0:T(8,128)S(1)}, f32[256,256]{1,0:T(8,128)S(1)}, u32[]{:S(2)}, u32[]{:S(2)}) collective-permute-start(f32[256,256]{1,0:T(8,128)S(1)} %get-tuple-element.32), channel_id=1, source_target_pairs={{0,1},{1,2},{2,3},{3,0},{4,5},{5,6},{6,7},{7,4},{8,9},{9,10},{10,1... | collective-permute-start | bytes 786440 | tf_op jit(solution)/shard_map/ppermute | solution.py:251
  5.1 20.4 %collective-permute-start.4 = (f32[256,256]{1,0:T(8,128)S(1)}, f32[256,256]{1,0:T(8,128)S(1)}, u32[]{:S(2)}, u32[]{:S(2)}) collective-permute-start(f32[256,256]{1,0:T(8,128)S(1)} %get-tuple-element.31), channel_id=1, source_target_pairs={{0,1},{1,2},{2,3},{3,0},{4,5},{5,6},{6,7},{7,4},{8,9},{9,10},{10,1... | collective-permute-start | bytes 786440 | tf_op jit(solution)/shard_map/ppermute | solution.py:251
  5.3 20.2 %collective-permute-start.5 = (f32[256,256]{1,0:T(8,128)S(1)}, f32[256,256]{1,0:T(8,128)S(1)}, u32[]{:S(2)}, u32[]{:S(2)}) collective-permute-start(f32[256,256]{1,0:T(8,128)S(1)} %get-tuple-element.32), channel_id=1, source_target_pairs={{0,3},{1,0},{2,1},{3,2},{4,7},{5,4},{6,5},{7,6},{8,11},{9,8},{10,9... | collective-permute-start | bytes 786440 | tf_op jit(solution)/shard_map/ppermute | solution.py:251
  7.8 1.0 %copy-start.2 = (f32[512,256]{1,0:T(8,128)S(1)}, f32[512,256]{1,0:T(8,128)}, u32[]{:S(2)}) copy-start(f32[512,256]{1,0:T(8,128)} %own.3) | copy-start | bytes 1572868
  9.6 4.0 %collective-permute-start.7 = (f32[32,8,128]{2,1,0:T(8,128)S(1)}, f32[32,8,128]{2,1,0:T(8,128)S(1)}, u32[]{:S(2)}, u32[]{:S(2)}) collective-permute-start(f32[32,8,128]{2,1,0:T(8,128)S(1)} %get-tuple-element.23), channel_id=1, source_target_pairs={{0,4},{4,0},{8,12},{12,8},{16,20},{20,16},{24,28},{28,24},{32,36},... | collective-permute-start | bytes 393224 | tf_op jit(solution)/shard_map/ppermute | solution.py:247
  12.1 18.9 %collective-permute-start.3 = (f32[256,256]{1,0:T(8,128)S(1)}, f32[256,256]{1,0:T(8,128)S(1)}, u32[]{:S(2)}, u32[]{:S(2)}) collective-permute-start(f32[256,256]{1,0:T(8,128)S(1)} %collective-permute-done.2.a2), channel_id=1, source_target_pairs={{0,3},{1,0},{2,1},{3,2},{4,7},{5,4},{6,5},{7,6},{8,11},{9,8},{10,9... | collective-permute-start | bytes 786440 | tf_op jit(solution)/shard_map/ppermute | solution.py:251
  13.5 17.5 %collective-permute-start.1 = (f32[256,256]{1,0:T(8,128)S(1)}, f32[256,256]{1,0:T(8,128)S(1)}, u32[]{:S(2)}, u32[]{:S(2)}) collective-permute-start(f32[256,256]{1,0:T(8,128)S(1)} %collective-permute-done.b1), channel_id=1, source_target_pairs={{0,1},{1,2},{2,3},{3,0},{4,5},{5,6},{6,7},{7,4},{8,9},{9,10},{10,1... | collective-permute-start | bytes 786440 | tf_op jit(solution)/shard_map/ppermute | solution.py:251
  14.3 21.3 %all-to-all-start = ((f32[32,8,128]{2,1,0:T(8,128)}), f32[32,8,128]{2,1,0:T(8,128)S(1)}, u32[]{:S(2)}, u32[]{:S(2)}) async-start(f32[32,8,128]{2,1,0:T(8,128)} %add.45), calls=%async_computation | async-start | bytes 262144 | tf_op jit(solution)/shard_map/all_to_all | solution.py:30
  25.5 2.2 %copy-start = (f32[2048,512]{1,0:T(8,128)S(1)}, f32[2048,512]{1,0:T(8,128)}, u32[]{:S(2)}) copy-start(f32[2048,512]{1,0:T(8,128)} %trailing.3) | copy-start | bytes 12582916
  27.7 1.0 %copy-start.3 = (f32[512,256]{1,0:T(8,128)S(1)}, f32[512,256]{1,0:T(8,128)}, u32[]{:S(2)}) copy-start(f32[512,256]{1,0:T(8,128)} %own.3) | copy-start | bytes 1572868
  32.2 10.3 %collective-permute-start.6 = (f32[32,16,128]{2,1,0:T(8,128)S(1)}, f32[32,16,128]{2,1,0:T(8,128)S(1)}, u32[]{:S(2)}, u32[]{:S(2)}) collective-permute-start(f32[32,16,128]{2,1,0:T(8,128)S(1)} %get-tuple-element.21), channel_id=1, source_target_pairs={{0,4},{4,0},{8,12},{12,8},{16,20},{20,16},{24,28},{28,24},{32,36},... | collective-permute-start | bytes 786440 | tf_op jit(solution)/shard_map/ppermute | solution.py:247
  35.6 4.3 %collective-permute-start.10 = (f32[8,128]{1,0:T(8,128)S(1)}, f32[8,128]{1,0:T(8,128)S(1)}, u32[]{:S(2)}, u32[]{:S(2)}) collective-permute-start(f32[8,128]{1,0:T(8,128)S(1)} %reduce_sum.18), channel_id=1, source_target_pairs={{0,3},{1,0},{2,1},{3,2},{4,7},{5,4},{6,5},{7,6},{8,11},{9,8},{10,9... | collective-permute-start | bytes 12296 | tf_op jit(solution)/shard_map/ppermute | solution.py:251
  38.6 3.7 %collective-permute-start.9 = (f32[8,128]{1,0:T(8,128)S(1)}, f32[8,128]{1,0:T(8,128)S(1)}, u32[]{:S(2)}, u32[]{:S(2)}) collective-permute-start(f32[8,128]{1,0:T(8,128)S(1)} %reduce_sum.18), channel_id=1, source_target_pairs={{0,1},{1,2},{2,3},{3,0},{4,5},{5,6},{6,7},{7,4},{8,9},{9,10},{10,1... | collective-permute-start | bytes 12296 | tf_op jit(solution)/shard_map/ppermute | solution.py:251
  38.6 4.0 %collective-permute-start.8 = (f32[8,128]{1,0:T(8,128)S(1)}, f32[8,128]{1,0:T(8,128)S(1)}, u32[]{:S(2)}, u32[]{:S(2)}) collective-permute-start(f32[8,128]{1,0:T(8,128)S(1)} %reduce_sum.18), channel_id=1, source_target_pairs={{0,2},{1,3},{2,0},{3,1},{4,6},{5,7},{6,4},{7,5},{8,10},{9,11},{10,... | collective-permute-start | bytes 12296 | tf_op jit(solution)/shard_map/ppermute | solution.py:251
  63.3 20.1 %all-to-all-start.2 = ((f32[32,16,128]{2,1,0:T(8,128)}), f32[32,16,128]{2,1,0:T(8,128)S(1)}, u32[]{:S(2)}, u32[]{:S(2)}) async-start(f32[32,16,128]{2,1,0:T(8,128)} %broadcast_in_dim.5), calls=%async_computation.2 | async-start | bytes 524288 | tf_op jit(solution)/shard_map/all_to_all | solution.py:30
  70.7 4.0 %collective-permute-start.11 = (f32[32,8,128]{2,1,0:T(8,128)S(1)}, f32[32,8,128]{2,1,0:T(8,128)S(1)}, u32[]{:S(2)}, u32[]{:S(2)}) collective-permute-start(f32[32,8,128]{2,1,0:T(8,128)S(1)} %slice.16), channel_id=1, source_target_pairs={{0,4},{4,0},{8,12},{12,8},{16,20},{20,16},{24,28},{28,24},{32,36},... | collective-permute-start | bytes 393224 | tf_op jit(solution)/shard_map/ppermute | solution.py:247
  83.5 4.0 %copy-start.1 = (f32[2048,512]{1,0:T(8,128)S(1)}, f32[2048,512]{1,0:T(8,128)}, u32[]{:S(2)}) copy-start(f32[2048,512]{1,0:T(8,128)} %trailing.3) | copy-start | bytes 12582916
  83.5 4.0 %copy-start.4 = (f32[512,256]{1,0:T(8,128)S(1)}, f32[512,256]{1,0:T(8,128)}, u32[]{:S(2)}) copy-start(f32[512,256]{1,0:T(8,128)} %own.3) | copy-start | bytes 1572868
  83.5 2.2 %collective-permute-start.12 = (f32[32,16,128]{2,1,0:T(8,128)S(1)}, f32[32,16,128]{2,1,0:T(8,128)S(1)}, u32[]{:S(2)}, u32[]{:S(2)}) collective-permute-start(f32[32,16,128]{2,1,0:T(8,128)S(1)} %all-to-all-done.2.mine), channel_id=1, source_target_pairs={{0,4},{4,0},{8,12},{12,8},{16,20},{20,16},{24,28},{28,24},{32,36},... | collective-permute-start | bytes 786440 | tf_op jit(solution)/shard_map/ppermute | solution.py:247
